TPU v7x, 32 devices: a whole 2x2x4 slice. The times are simulated.
32 devices in a mesh: group: 4 (over y, core), rep: 8 (over z, x).
Axes of the slice: x: 2, y: 2, z: 4, core: 2. Of those that a mesh axis runs over, the one named last changes fastest.
Arguments:
- table_hot: bfloat16 [32768, 512], P(('group', 'rep')), may hold values from -6 to 6
- table_mid: bfloat16 [131072, 128], P(('group', 'rep')), may hold values from -6 to 6
- table_cold: bfloat16 [131072, 128], P(('group', 'rep')), may hold values from -6 to 6
- proj_hot: bfloat16 [512, 256], replicated, may hold values from -0.25 to 0.25
- proj_mid: bfloat16 [128, 256], replicated, may hold values from -0.5 to 0.5
- proj_cold: bfloat16 [32, 256], replicated, may hold values from -1 to 1
- tower_in: bfloat16 [256, 1024], replicated, may hold values from -0.375 to 0.375
- tower_out: bfloat16 [1024, 256], replicated, may hold values from -0.1875 to 0.1875
- queries: bfloat16 [16384, 256], P(('group', 'rep')), may hold values from -68 to 68
- labels: int32 [16384], P(('group', 'rep')), may hold values from 0 to 4095
- item_slot: int32 [32, 4, 1024], P(('group', 'rep')), may hold values from 0 to 255
- item_block: int32 [32, 4, 1024], P(('group', 'rep')), may hold values from 0 to 2
- serve_rows: int32 [32, 3, 256], P(('group', 'rep')), may hold values from 0 to 16383, as said below
Outputs:
- query_loss: float32 [16384], P(('group', 'rep'))
- query_grad: float32 [16384, 256], P(('group', 'rep'))
- grad_hot: float32 [32768, 512], P(('group', 'rep'))
- grad_mid: float32 [131072, 128], P(('group', 'rep'))
- grad_cold: float32 [131072, 128], P(('group', 'rep'))
- grad_proj_hot: float32 [512, 256], P(None, 'rep')
- grad_proj_mid: float32 [128, 256], P(None, 'rep')
- grad_proj_cold: float32 [32, 256], P(None, 'rep')
- grad_tower_in: float32 [256, 1024], P(None, 'rep')
- grad_tower_out: float32 [1024, 256], P(None, 'rep')
Inputs may be any that keep to these rules, and one draw needn't show every extreme that they name: serve_rows[o, b, d * 8 + c] is a row of owner o's shard of block b that requester d sees in slot c; for block 0 it is below 1024, for block 1 below 4096, for block 2 below 16384; the 8 rows that one owner serves to one requester in one block are distinct.
All inputs are finite; a program needn't handle non-finite values.
Results may differ from a plain program's by a relative error of at most 0.02.
The roundings to bfloat16 on the way count: a program that leaves them out, or rounds other values in their place, can miss the bound.
Values may be sent and summed in bfloat16 or wider, within the bound.
No kernel may reach another device: no remote copies, remote signals or barrier semaphores. Data moves between devices by JAX's collectives and lax.ppermute only.
A program may use at most 128 MiB of HBM per device.

v0:
```python
import jax
import jax.numpy as jnp
from jax import lax
from jax.sharding import PartitionSpec as P

NORM_EPS = 1e-06
LOGIT_SCALE = 0.2


def merged(value, axis, join):
    pieces = jax.tree.map(lambda part: lax.all_gather(part, axis), value)
    head = jax.tree.map(lambda part: part[0], pieces)
    tail = jax.tree.map(lambda part: part[1:], pieces)
    total, _ = lax.scan(lambda total, piece: (join(total, piece), None), head, tail)
    return total


def silu_slope(pre_act):
    sigmoid = jax.nn.sigmoid(pre_act)
    return sigmoid * (1.0 + pre_act * (1.0 - sigmoid))


def pick_cold(cold_lines, row_ids, col_width):
    pieces = cold_lines.reshape(cold_lines.shape[0], 4, col_width)
    select = lax.broadcasted_iota(jnp.int32, (row_ids.shape[0], 4), 1) == (row_ids % 4)[:, None]
    return jnp.sum(jnp.where(select[:, :, None], pieces, jnp.zeros((), pieces.dtype)), axis=1)


def cold_add(row_ids, values, line_shape):
    select = (
        lax.broadcasted_iota(jnp.int32, (row_ids.shape[0], 4), 1) == (row_ids % 4)[:, None]
    ).astype(jnp.float32)
    spread = (select[:, :, None] * values[:, None, :]).reshape(row_ids.shape[0], line_shape[1])
    return jnp.zeros(line_shape, jnp.float32).at[row_ids // 4].add(spread)


def project(raw_rows, weight):
    return jnp.dot(raw_rows, weight, preferred_element_type=jnp.float32).astype(jnp.bfloat16)


def unproject(slot_grad, weight):
    return lax.dot_general(
        slot_grad, weight, (((1,), (1,)), ((), ())), preferred_element_type=jnp.float32
    )


def contract(left_rows, right_rows):
    return lax.dot_general(
        left_rows, right_rows, (((0,), (0,)), ((), ())), preferred_element_type=jnp.float32
    )


def combine_totals(earlier, later):
    joint_max = jnp.maximum(earlier[0], later[0])
    joint_sum = earlier[1] * jnp.exp(earlier[0] - joint_max) + later[1] * jnp.exp(
        later[0] - joint_max
    )
    return (joint_max, joint_sum, earlier[2] + later[2])


def local(
    table_hot,
    table_mid,
    table_cold,
    proj_hot,
    proj_mid,
    proj_cold,
    tower_in,
    tower_out,
    queries,
    labels,
    item_slot,
    item_block,
    serve_rows,
):
    devices = lax.axis_size(("group", "rep"))
    served = serve_rows[0]
    slot_total = served.shape[1]
    slots_each = slot_total // devices
    cold_width = proj_cold.shape[0]
    width_model = tower_in.shape[0]
    item_count = item_slot.shape[2]
    field_count = item_slot.shape[1]
    rows_hot = table_hot[served[0]]
    rows_mid = table_mid[served[1]]
    rows_cold = pick_cold(table_cold[served[2] // 4], served[2], cold_width)
    first_block = rows_hot.reshape(devices, slots_each, rows_hot.shape[1])
    got_first, got_mid, got_cold = (
        lax.all_to_all(first_block, ("group", "rep"), split_axis=0, concat_axis=0, tiled=True),
        lax.all_to_all(
            rows_mid.reshape(devices, slots_each, rows_mid.shape[1]),
            ("group", "rep"),
            split_axis=0,
            concat_axis=0,
            tiled=True,
        ),
        lax.all_to_all(
            rows_cold.reshape(devices, slots_each // 4, 4 * cold_width),
            ("group", "rep"),
            split_axis=0,
            concat_axis=0,
            tiled=True,
        ),
    )
    raw_mid = got_mid.reshape(slot_total, rows_mid.shape[1])
    raw_cold = got_cold.reshape(slot_total, cold_width)
    raw_hot = got_first.reshape(slot_total, rows_hot.shape[1])
    near_hot = project(raw_hot, proj_hot)
    slot_table = jnp.concatenate(
        [near_hot, project(raw_mid, proj_mid), project(raw_cold, proj_cold)], axis=0
    )
    slot_index = item_block[0] * slot_total + item_slot[0]
    pooled = jnp.sum(slot_table[slot_index].astype(jnp.float32), axis=0).astype(jnp.bfloat16)
    pre_act = jnp.dot(pooled, tower_in, preferred_element_type=jnp.float32)
    hidden = jax.nn.silu(pre_act).astype(jnp.bfloat16)
    residual = pooled.astype(jnp.float32) + jnp.dot(
        hidden, tower_out, preferred_element_type=jnp.float32
    )
    inv_rms = lax.rsqrt(jnp.mean(residual * residual, axis=1, keepdims=True) + NORM_EPS)
    vectors = (residual * inv_rms).astype(jnp.bfloat16)
    group_queries = lax.all_gather(queries, "group", axis=0, tiled=True)
    group_labels = lax.all_gather(labels, "group", axis=0, tiled=True)
    scores = (
        lax.dot_general(
            group_queries, vectors, (((1,), (1,)), ((), ())), preferred_element_type=jnp.float32
        )
        * LOGIT_SCALE
    )
    group_at = lax.axis_index("group")
    columns = group_at * item_count + lax.broadcasted_iota(jnp.int32, scores.shape, 1)
    onehot = columns == group_labels[:, None]
    local_max = jnp.max(scores, axis=1)
    local_total = jnp.sum(jnp.exp(scores - local_max[:, None]), axis=1)
    local_pick = jnp.sum(jnp.where(onehot, scores, 0.0), axis=1)
    joint_max, joint_sum, picked = merged(
        (local_max, local_total, local_pick), "group", combine_totals
    )
    log_total = joint_max + jnp.log(joint_sum)
    score_grad = (jnp.exp(scores - log_total[:, None]) - onehot.astype(jnp.float32)).astype(
        jnp.bfloat16
    )
    vec_grad = LOGIT_SCALE * contract(score_grad, group_queries)
    query_grad = lax.psum_scatter(
        (LOGIT_SCALE * jnp.dot(score_grad, vectors, preferred_element_type=jnp.float32)).astype(
            jnp.bfloat16
        ),
        "group",
        scatter_dimension=0,
        tiled=True,
    ).astype(jnp.float32)
    query_loss = lax.dynamic_slice_in_dim(
        log_total - picked, group_at * queries.shape[0], queries.shape[0], 0
    )
    dot_wide = jnp.sum(vec_grad * residual, axis=1, keepdims=True)
    wide_grad = inv_rms * vec_grad - inv_rms**3 / width_model * residual * dot_wide
    wide_low = wide_grad.astype(jnp.bfloat16)
    hidden_grad = unproject(wide_low, tower_out)
    pre_grad = (hidden_grad * silu_slope(pre_act)).astype(jnp.bfloat16)
    pooled_grad = (unproject(pre_grad, tower_in) + wide_grad).astype(jnp.bfloat16)
    stacked = jnp.broadcast_to(
        pooled_grad.astype(jnp.float32)[None], (field_count, item_count, width_model)
    ).reshape(-1, width_model)
    slot_grad = jax.ops.segment_sum(
        stacked, slot_index.reshape(-1), num_segments=3 * slot_total
    ).astype(jnp.bfloat16)
    grad_hot_slots = slot_grad[:slot_total]
    grad_mid_slots = slot_grad[slot_total : 2 * slot_total]
    grad_cold_slots = slot_grad[2 * slot_total :]
    grad_ph = contract(raw_hot, grad_hot_slots)
    back_hot, back_mid, back_cold = (
        lax.all_to_all(
            unproject(grad_hot_slots, proj_hot)
            .reshape(devices, slots_each, rows_hot.shape[1])
            .astype(jnp.bfloat16),
            ("group", "rep"),
            split_axis=0,
            concat_axis=0,
            tiled=True,
        ).astype(jnp.float32),
        lax.all_to_all(
            unproject(grad_mid_slots, proj_mid)
            .reshape(devices, slots_each, rows_mid.shape[1])
            .astype(jnp.bfloat16),
            ("group", "rep"),
            split_axis=0,
            concat_axis=0,
            tiled=True,
        ).astype(jnp.float32),
        lax.all_to_all(
            unproject(grad_cold_slots, proj_cold)
            .reshape(devices, slots_each // 4, 4 * cold_width)
            .astype(jnp.bfloat16),
            ("group", "rep"),
            split_axis=0,
            concat_axis=0,
            tiled=True,
        ).astype(jnp.float32),
    )
    back_hot = back_hot.reshape(slot_total, rows_hot.shape[1])
    grad_pm = contract(raw_mid, grad_mid_slots)
    grad_pc = contract(raw_cold, grad_cold_slots)
    grad_hot = jnp.zeros(table_hot.shape, jnp.float32).at[served[0]].add(back_hot)
    grad_mid = (
        jnp.zeros(table_mid.shape, jnp.float32)
        .at[served[1]]
        .add(back_mid.reshape(slot_total, rows_mid.shape[1]))
    )
    grad_cold = cold_add(served[2], back_cold.reshape(slot_total, cold_width), table_cold.shape)
    grad_in_local = contract(pooled, pre_grad)
    grad_out_local = contract(hidden, wide_low)
    totals = lax.psum((grad_ph, grad_pm, grad_pc, grad_in_local, grad_out_local), ("group", "rep"))
    rep_count = lax.axis_size("rep")
    rep_at = lax.axis_index("rep")
    summed = tuple(
        (
            lax.dynamic_slice_in_dim(
                full_sum,
                rep_at * (full_sum.shape[1] // rep_count),
                full_sum.shape[1] // rep_count,
                1,
            )
            for full_sum in totals
        )
    )
    return (
        query_loss,
        query_grad,
        grad_hot,
        grad_mid,
        grad_cold,
        summed[0],
        summed[1],
        summed[2],
        summed[3],
        summed[4],
    )


def solution(mesh):
    return jax.shard_map(
        local,
        mesh=mesh,
        in_specs=(
            P(("group", "rep"), None),
            P(("group", "rep"), None),
            P(("group", "rep"), None),
            P(),
            P(),
            P(),
            P(),
            P(),
            P(("group", "rep"), None),
            P(("group", "rep")),
            P(("group", "rep"), None, None),
            P(("group", "rep"), None, None),
            P(("group", "rep"), None, None),
        ),
        out_specs=(
            P(("group", "rep")),
            P(("group", "rep"), None),
            P(("group", "rep"), None),
            P(("group", "rep"), None),
            P(("group", "rep"), None),
            P(None, "rep"),
            P(None, "rep"),
            P(None, "rep"),
            P(None, "rep"),
            P(None, "rep"),
        ),
        check_vma=False,
    )
```

profile of v0, /device:TPU:0, one launch (start us, length us, event | category | flops | bytes accessed | tf_op | source)
XLA Modules:
  0.0 317.8 jit_solution(5360440472956101922)
XLA Ops:
  13.1 7.3 %all-to-all-start.2 = ((bf16[32,2,128]{2,1,0:T(2,128)(2,1)}), bf16[32,2,128]{2,1,0:T(2,128)(2,1)S(1)}, u32[]{:S(2)}, u32[]{:S(2)}) async-start(bf16[32,2,128]{2,1,0:T(2,128)(2,1)} %reshape.345), calls=%async_computation.2 | async-start | bytes 32768 | tf_op jit(solution)/shard_map/all_to_all | solution.py:97
  22.0 2.7 gather_fusion.1
  27.5 4.9 %all-to-all-start.1 = ((bf16[32,8,128]{2,1,0:T(8,128)(2,1)}), bf16[32,8,128]{2,1,0:T(8,128)(2,1)S(1)}, u32[]{:S(2)}, u32[]{:S(2)}) async-start(bf16[32,8,128]{2,1,0:T(8,128)(2,1)} %bitcast.9), calls=%async_computation.1 | async-start | bytes 131072 | tf_op jit(solution)/shard_map/all_to_all | solution.py:90
  33.0 6.7 %all-to-all-done.1 = bf16[32,8,128]{2,1,0:T(8,128)(2,1)S(1)} async-done(((bf16[32,8,128]{2,1,0:T(8,128)(2,1)}), bf16[32,8,128]{2,1,0:T(8,128)(2,1)S(1)}, u32[]{:S(2)}, u32[]{:S(2)}) %all-to-all-start.1) | async-done | bytes 65568 | tf_op jit(solution)/shard_map/all_to_all | solution.py:90
  42.9 5.2 %all-gather.3 = s32[4,1,512]{2,1,0:T(1,128)S(1)} all-gather(s32[1,1,512]{2,1,0:T(1,128)S(1)} %bitcast.126), channel_id=1, replica_groups=mesh['group'=4,'rep'=8] {'group'}, dimensions={0}, use_global_device_ids=true | all-gather | bytes 10240 | tf_op jit(solution)/shard_map/all_gather | solution.py:122
  48.6 4.1 %all-to-all-done = bf16[32,8,512]{2,1,0:T(8,128)(2,1)S(1)} async-done(((bf16[32,8,512]{2,1,0:T(8,128)(2,1)}), bf16[32,8,512]{2,1,0:T(8,128)(2,1)S(1)}, u32[]{:S(2)}, u32[]{:S(2)}) %all-to-all-start) | async-done | bytes 262176 | tf_op jit(solution)/shard_map/all_to_all | solution.py:89
  53.4 16.6 %gather_fusion.3 = bf16[4096,256]{1,0:T(8,128)(2,1)S(1)} fusion(bf16[768,256]{1,0:T(8,128)(2,1)S(1)} %pad_maximum_fusion, s32[4096]{0:T(1024)} %bitcast_clamp_fusion), kind=kCustom, calls=%fused_computation.3 | custom fusion | bytes 4210688 | tf_op jit(solution)/shard_map/gather | solution.py:113
  72.5 4.5 %multiply_convert_fusion.1 = (bf16[1024,1024]{1,0:T(8,128)(2,1)S(1)}, f32[1024,1024]{1,0:T(8,128)}) fusion(bf16[1024,256]{1,0:T(8,128)(2,1)} %reduce_sum.61, bf16[256,1024]{1,0:T(8,128)(2,1)} %param.21), kind=kOutput, calls=%fused_computation.24 | convolution fusion | flops 542113792 | bytes 7340032 | tf_op jit(solution)/shard_map/dot_general | solution.py:114
  81.7 5.2 %all-gather = f32[8192]{0:T(1024)S(1)} all-gather(f32[2048]{0:T(1024)S(1)} %get-tuple-element.88), channel_id=2, replica_groups=mesh['group'=4,'rep'=8] {'group'}, dimensions={0}, use_global_device_ids=true | all-gather | bytes 40960 | tf_op jit(solution)/shard_map/all_gather | solution.py:11
  89.6 5.2 %all-gather.1 = f32[8192]{0:T(1024)S(1)} all-gather(f32[2048]{0:T(1024)S(1)} %get-tuple-element.53), channel_id=3, replica_groups=mesh['group'=4,'rep'=8] {'group'}, dimensions={0}, use_global_device_ids=true | all-gather | bytes 40960 | tf_op jit(solution)/shard_map/all_gather | solution.py:11
  94.8 5.4 %all-gather.2 = f32[8192]{0:T(1024)S(1)} all-gather(f32[2048]{0:T(1024)S(1)} %get-tuple-element.52), channel_id=4, replica_groups=mesh['group'=4,'rep'=8] {'group'}, dimensions={0}, use_global_device_ids=true | all-gather | bytes 40960 | tf_op jit(solution)/shard_map/all_gather | solution.py:11
  100.6 4.8 %fusion.2 = bf16[2048,1024]{0,1:T(8,128)(2,1)S(1)} fusion(f32[1024,2048]{1,0:T(8,128)} %copy-done.1, f32[2048]{0:T(1024)S(1)} %log_add_fusion, s32[2048]{0:T(1024)} %bitcast.117, s32[1024]{0:T(1024)S(1)} %iota_add_fusion), kind=kLoop, calls=%fused_computation.16 | loop fusion | flops 12582912 | bytes 12603392 | tf_op jit(solution)/shard_map/convert_element_type | solution.py:139
  117.0 3.5 %broadcast_in_dim.27 = f32[4,1024,256]{2,1,0:T(8,128)} broadcast(f32[1024,256]{1,0:T(8,128)} %copy.35), dimensions={1,2} | broadcast | bytes 5242880 | tf_op jit(solution)/shard_map/broadcast_in_dim | solution.py:160
  120.5 23.0 %scatter_custom_fusion = f32[768,256]{1,0:T(8,128)S(1)} fusion(s32[4096]{0:T(1024)} %bitcast.118, f32[4096,256]{1,0:T(8,128)} %bitcast.110, f32[]{:T(128)} %constant.85.clone.1), kind=kCustom, calls=%fused_computation.52 | custom fusion | flops 1048576 | bytes 786944 | tf_op jit(solution)/shard_map/scatter-add | solution.py:163
  146.5 4.6 %fusion.6 = bf16[2048,256]{1,0:T(8,128)(2,1)} fusion(bf16[2048,1024]{0,1:T(8,128)(2,1)} %copy-done.5, f32[1024,256]{0,1:T(8,128)S(1)} %get-tuple-element.87, f32[1024]{0:T(1024)S(1)} %get-tuple-element.78), kind=kOutput, calls=%fused_computation.27 | convolution fusion | flops 1075314688 | bytes 6295552 | tf_op jit(solution)/shard_map/dot_general | solution.py:144
  152.2 2.8 all-to-all-start.5
  155.8 6.2 %all-to-all-done.5 = bf16[32,2,128]{2,1,0:T(2,128)(2,1)S(1)} async-done(((bf16[32,2,128]{2,1,0:T(2,128)(2,1)}), bf16[32,2,128]{2,1,0:T(2,128)(2,1)S(1)}, u32[]{:S(2)}, u32[]{:S(2)}) %all-to-all-start.5) | async-done | bytes 16416 | tf_op jit(solution)/shard_map/all_to_all | solution.py:189
  165.6 6.8 %all-to-all-done.4 = bf16[32,8,128]{2,1,0:T(8,128)(2,1)S(1)} async-done(((bf16[32,8,128]{2,1,0:T(8,128)(2,1)}), bf16[32,8,128]{2,1,0:T(8,128)(2,1)S(1)}, u32[]{:S(2)}, u32[]{:S(2)}) %all-to-all-start.4) | async-done | bytes 65568 | tf_op jit(solution)/shard_map/all_to_all | solution.py:180
  175.1 40.7 %psum.37 = f32[32,256]{1,0:T(8,128)S(1)} all-reduce(f32[32,256]{1,0:T(8,128)S(1)} %fusion.27), channel_id=1, replica_groups=mesh['group'=4,'rep'=8] {'group','rep'}, use_global_device_ids=true, to_apply=%region_16.17 | all-reduce | flops 8192 | bytes 65536 | tf_op jit(solution)/shard_map/psum | solution.py:211
  218.1 3.0 scatter_custom_fusion.3
  221.1 3.0 scatter_custom_fusion.2
  224.0 3.7 %scatter_custom_fusion.1 = f32[1024,512]{1,0:T(8,128)} fusion(s32[256]{0:T(256)} %bitcast.120, f32[]{:T(128)} %constant.85.clone.1, bf16[32,8,512]{2,1,0:T(8,128)(2,1)S(1)} %all-to-all-done.3), kind=kCustom, calls=%fused_computation.46 | custom fusion | flops 262144 | bytes 2359808 | tf_op jit(solution)/shard_map/scatter-add | solution.py:202
  227.7 55.6 %all-reduce.3.cloned.1.call-done = (f32[512,256]{0,1:T(8,128)}, f32[128,256]{0,1:T(8,128)}, f32[256,1024]{1,0:T(8,128)}, f32[1024,256]{0,1:T(8,128)}) async-done(((f32[512,256]{0,1:T(8,128)}, f32[128,256]{0,1:T(8,128)}, f32[256,1024]{1,0:T(8,128)}, f32[1024,256]{0,1:T(8,128)}), (f32[512,256]{0,1:T(8,128)}, f32[128,256]{0,1:T(8,128)}, f32[256,1024]{1,0:T(8,128)}, ...) | async-done | bytes 2752528 | tf_op jit(solution)/shard_map/psum | solution.py:211
  289.2 20.4 %reduce-scatter.2.cloned.1.call-done = bf16[512,256]{1,0:T(8,128)(2,1)} async-done(((bf16[2048,256]{1,0:T(8,128)(2,1)}), bf16[512,256]{1,0:T(8,128)(2,1)}) %reduce-scatter.2.cloned.1.call-update) | async-done | bytes 262160 | tf_op jit(solution)/shard_map/reduce_scatter | solution.py:143
  (147 shorter events, 58.0 us)
Async XLA Ops:
  7.2 17.5 %copy-start = (bf16[1024,512]{1,0:T(8,128)(2,1)S(1)}, bf16[1024,512]{1,0:T(8,128)(2,1)}, u32[]{:S(2)}) copy-start(bf16[1024,512]{1,0:T(8,128)(2,1)} %param.15) | copy-start | bytes 3145732
  7.2 35.7 %copy-start.26 = (s32[512]{0:T(512)S(1)}, s32[512]{0:T(512)}, u32[]{:S(2)}) copy-start(s32[512]{0:T(512)} %param.24) | copy-start | bytes 6148
  7.2 41.0 %copy-start.20 = (bf16[32,256]{1,0:T(8,128)(2,1)S(1)}, bf16[32,256]{1,0:T(8,128)(2,1)}, u32[]{:S(2)}) copy-start(bf16[32,256]{1,0:T(8,128)(2,1)} %param.20) | copy-start | bytes 49156
  7.2 41.2 %copy-start.16 = (bf16[128,256]{1,0:T(8,128)(2,1)S(1)}, bf16[128,256]{1,0:T(8,128)(2,1)}, u32[]{:S(2)}) copy-start(bf16[128,256]{1,0:T(8,128)(2,1)} %param.19) | copy-start | bytes 196612
  7.2 45.5 %copy-start.9 = (bf16[512,256]{1,0:T(8,128)(2,1)S(1)}, bf16[512,256]{1,0:T(8,128)(2,1)}, u32[]{:S(2)}) copy-start(bf16[512,256]{1,0:T(8,128)(2,1)} %param.18) | copy-start | bytes 786436
  7.2 71.9 %all-gather.6.cloned.1.call-start = ((), (), s32[]{:S(2)}) async-start(), calls=%async_computation.7 | async-start | bytes 1310720 | tf_op jit(solution)/shard_map/all_gather | solution.py:121
  8.7 13.2 %copy-start.24 = (s32[256,1]{0,1:T(1,128)}, s32[256,1]{0,1:T(1,128)S(1)}, u32[]{:S(2)}) copy-start(s32[256,1]{0,1:T(1,128)S(1)} %get-tuple-element.81) | copy-start | bytes 3076
  8.7 34.2 %copy-start.23 = (s32[256,1]{0,1:T(1,128)}, s32[256,1]{0,1:T(1,128)S(1)}, u32[]{:S(2)}) copy-start(s32[256,1]{0,1:T(1,128)S(1)} %get-tuple-element.79) | copy-start | bytes 3076
  13.1 14.4 %all-to-all-start.2 = ((bf16[32,2,128]{2,1,0:T(2,128)(2,1)}), bf16[32,2,128]{2,1,0:T(2,128)(2,1)S(1)}, u32[]{:S(2)}, u32[]{:S(2)}) async-start(bf16[32,2,128]{2,1,0:T(2,128)(2,1)} %reshape.345), calls=%async_computation.2 | async-start | bytes 32768 | tf_op jit(solution)/shard_map/all_to_all | solution.py:97
  27.5 12.2 %all-to-all-start.1 = ((bf16[32,8,128]{2,1,0:T(8,128)(2,1)}), bf16[32,8,128]{2,1,0:T(8,128)(2,1)S(1)}, u32[]{:S(2)}, u32[]{:S(2)}) async-start(bf16[32,8,128]{2,1,0:T(8,128)(2,1)} %bitcast.9), calls=%async_computation.1 | async-start | bytes 131072 | tf_op jit(solution)/shard_map/all_to_all | solution.py:90
  39.7 13.3 %copy-start.13 = (bf16[32,8,128]{2,1,0:T(8,128)(2,1)}, bf16[32,8,128]{2,1,0:T(8,128)(2,1)S(1)}, u32[]{:S(2)}) copy-start(bf16[32,8,128]{2,1,0:T(8,128)(2,1)S(1)} %all-to-all-done.1) | copy-start | bytes 196612
  39.7 13.0 %all-to-all-start = ((bf16[32,8,512]{2,1,0:T(8,128)(2,1)}), bf16[32,8,512]{2,1,0:T(8,128)(2,1)S(1)}, u32[]{:S(2)}, u32[]{:S(2)}) async-start(bf16[32,8,512]{2,1,0:T(8,128)(2,1)} %bitcast.5), calls=%async_computation | async-start | bytes 524288 | tf_op jit(solution)/shard_map/all_to_all | solution.py:89
  42.3 241.0 %all-reduce.3.cloned.1.call-start = ((), (), s32[]{:S(2)}) async-start(), calls=%async_computation.9 | async-start | bytes 5505024 | tf_op jit(solution)/shard_map/psum | solution.py:211
  48.1 38.8 %copy-start.18 = (s32[4,1,512]{2,1,0:T(1,128)}, s32[4,1,512]{2,1,0:T(1,128)S(1)}, u32[]{:S(2)}) copy-start(s32[4,1,512]{2,1,0:T(1,128)S(1)} %all-gather.3) | copy-start | bytes 24580
  81.7 7.9 %copy-start.1 = (f32[1024,2048]{1,0:T(8,128)}, f32[1024,2048]{1,0:T(8,128)S(1)}, u32[]{:S(2)}) copy-start(f32[1024,2048]{1,0:T(8,128)S(1)} %get-tuple-element.89) | copy-start | bytes 25165828
  115.6 27.9 %copy-start.7 = (bf16[32,8,512]{2,1,0:T(8,128)(2,1)S(1)}, bf16[32,8,512]{2,1,0:T(8,128)(2,1)}, u32[]{:S(2)}) copy-start(bf16[32,8,512]{2,1,0:T(8,128)(2,1)} %copy-done.6) | copy-start | bytes 786436
  146.4 8.5 %copy-start.17 = (bf16[128,256]{1,0:T(8,128)(2,1)S(1)}, bf16[128,256]{1,0:T(8,128)(2,1)}, u32[]{:S(2)}) copy-start(bf16[128,256]{1,0:T(8,128)(2,1)} %param.19) | copy-start | bytes 196612
  146.4 18.2 %copy-start.10 = (bf16[512,256]{1,0:T(8,128)(2,1)S(1)}, bf16[512,256]{1,0:T(8,128)(2,1)}, u32[]{:S(2)}) copy-start(bf16[512,256]{1,0:T(8,128)(2,1)} %param.18) | copy-start | bytes 786436
  146.4 28.5 %copy-start.12 = (bf16[256,32]{1,0:T(8,128)(2,1)S(1)}, bf16[256,32]{1,0:T(8,128)(2,1)}, u32[]{:S(2)}) copy-start(bf16[256,32]{1,0:T(8,128)(2,1)} %copy-done.11) | copy-start | bytes 49156
  146.5 71.5 %copy-start.22 = (f32[256,4]{0,1:T(4,128)S(1)}, f32[256,4]{0,1:T(4,128)}, u32[]{:S(2)}) copy-start(f32[256,4]{0,1:T(4,128)} %get-tuple-element.82) | copy-start | bytes 12292
  146.5 163.1 %reduce-scatter.2.cloned.1.call-start = ((), (), s32[]{:S(2)}) async-start(), calls=%async_computation.8 | async-start | bytes 1310720 | tf_op jit(solution)/shard_map/reduce_scatter | solution.py:143
  152.2 9.8 %all-to-all-start.5 = ((bf16[32,2,128]{2,1,0:T(2,128)(2,1)}), bf16[32,2,128]{2,1,0:T(2,128)(2,1)S(1)}, u32[]{:S(2)}, u32[]{:S(2)}) async-start(bf16[32,2,128]{2,1,0:T(2,128)(2,1)} %convert_element_type.98), calls=%async_computation.6 | async-start | bytes 32768 | tf_op jit(solution)/shard_map/all_to_all | solution.py:189
  162.0 10.3 %all-to-all-start.4 = ((bf16[32,8,128]{2,1,0:T(8,128)(2,1)}), bf16[32,8,128]{2,1,0:T(8,128)(2,1)S(1)}, u32[]{:S(2)}, u32[]{:S(2)}) async-start(bf16[32,8,128]{2,1,0:T(8,128)(2,1)} %fusion.10), calls=%async_computation.5 | async-start | bytes 131072 | tf_op jit(solution)/shard_map/all_to_all | solution.py:180
  172.3 51.7 %all-to-all-start.3 = ((bf16[32,8,512]{2,1,0:T(8,128)(2,1)}), bf16[32,8,512]{2,1,0:T(8,128)(2,1)S(1)}, u32[]{:S(2)}, u32[]{:S(2)}) async-start(bf16[32,8,512]{2,1,0:T(8,128)(2,1)} %fusion.9), calls=%async_computation.4 | async-start | bytes 524288 | tf_op jit(solution)/shard_map/all_to_all | solution.py:171
  (13 other events, 43.0 us)
Sparse Core Ops, SparseCore 0:
  9.6 19.5 all-gather.5
  146.5 136.6 all-reduce.2
  285.8 23.7 reduce-scatter.1
where the time goes:
time: 319 us; the launch traced here: 318 us
  waiting for transfers between devices  101 us (32%)
  blocking collectives  61.6 us (19%)
  other arithmetic  48.3 us (15%)
  local copies, waits for them, and re-layouts  43.6 us (14%)
  matrix products  25.5 us (8%)
  starting transfers between devices  22.8 us (7%)
  between operations  14.4 us (5%)
    psum x1, waiting for transfers between devices, local(): lax.psum((grad_ph, grad_pm, grad_pc, grad_in_local, grad_out_local), ('gr...  55.6 us
    psum x1, blocking collectives, local(): lax.psum((grad_ph, grad_pm, grad_pc, grad_in_local, grad_out_local), ('gr...  40.7 us
    scatter-add x1, other arithmetic, local(): jax.ops.segment_sum(stacked, slot_index.reshape(-1), num_segments=3 * slo...  23 us
    reduce_scatter x1, waiting for transfers between devices, local(): lax.psum_scatter((LOGIT_SCALE * jnp.dot(score_grad, vectors, preferred_el...  20.4 us
    gather x1, local copies, waits for them, and re-layouts, local(): slot_table[slot_index].astype(jnp.float32)  16.6 us
    all_gather x3, blocking collectives, merged(): pieces = jax.tree.map(lambda part: lax.all_gather(part, axis), value)  15.7 us
    dot_general x6, matrix products, contract(): lax.dot_general(left_rows, right_rows, (((0,), (0,)), ((), ())), preferre...  7.8 us
    all_to_all x1, starting transfers between devices, local(): lax.all_to_all(rows_cold.reshape(devices, slots_each // 4, 4 * cold_width...  7.32 us
  transfers between devices with their start and end apart: 9, of which 7 were waited for; matrix products, arithmetic and copies ran while one was open for 20% of the time, Pallas kernels for 0%

commit v1 on v0

v1 whole, which is shorter than its diff:
```python
import functools

import jax
import jax.numpy as jnp
from jax import lax
from jax.experimental import pallas as pl
from jax.experimental.pallas import tpu as pltpu
from jax.sharding import PartitionSpec as P

NORM_EPS = 1e-06
LOGIT_SCALE = 0.2
AXES = ("group", "rep")
LANES = 128
QB = 256
IB = 256
MIB = 1 << 20
F32 = jnp.float32
BF16 = jnp.bfloat16

NN = (((1,), (0,)), ((), ()))
NT = (((1,), (1,)), ((), ()))
TN = (((0,), (0,)), ((), ()))


def mm(left, right, dims=NN):
    return lax.dot_general(left, right, dims, preferred_element_type=F32)


def ones_where(mask):
    return jnp.where(mask, jnp.float32(1), jnp.float32(0))


def iota(shape, dim):
    return lax.broadcasted_iota(jnp.int32, shape, dim)


def call(body, out_shape, inputs, scratch=(), vmem=40, name=None):
    spec = pl.BlockSpec(memory_space=pltpu.VMEM)
    return pl.pallas_call(
        body,
        out_shape=out_shape,
        in_specs=[spec] * len(inputs),
        out_specs=jax.tree.map(lambda _: spec, out_shape),
        scratch_shapes=list(scratch),
        compiler_params=pltpu.CompilerParams(vmem_limit_bytes=vmem * MIB),
        name=name,
    )(*inputs)


def sds(shape, dtype):
    return jax.ShapeDtypeStruct(shape, dtype)


def columns_of(rows_ref, pad_ref):
    pad_ref[...] = jnp.zeros_like(pad_ref)
    pad_ref[0 : rows_ref.shape[1], :] = rows_ref[0]
    return pad_ref[...].T


def gather_body(steps, cold_width, served, hot, mid, cold, out, pad, idx, acc):
    step = pl.program_id(0)
    slots = idx.shape[0]
    w_hot, w_mid = hot.shape[1], mid.shape[1]

    @pl.when(step == 0)
    def _():
        idx[...] = columns_of(served, pad)
        acc[...] = jnp.zeros_like(acc)

    def pick(table, col, at):
        block = table.shape[0]
        hit = iota((slots, block), 1) + step * block == col
        acc[:, at : at + table.shape[1]] += mm(ones_where(hit).astype(BF16), table[...])

    pick(hot, idx[:, 0:1], 0)
    pick(mid, idx[:, 1:2], w_hot)
    pick(cold, lax.shift_right_logical(idx[:, 2:3], 2), w_hot + w_mid)

    @pl.when(step == steps - 1)
    def _():
        out[:, 0 : w_hot + w_mid] = acc[:, 0 : w_hot + w_mid].astype(BF16)
        lines = acc[:, w_hot + w_mid :]
        mine = lax.div(iota(lines.shape, 1), cold_width) == (idx[:, 2:3] & 3)
        out[:, w_hot + w_mid :] = jnp.where(mine, lines, 0.0).astype(BF16)


def gather_rows(serve_rows, table_hot, table_mid, table_cold, cold_width):
    slots = serve_rows.shape[2]
    width = table_hot.shape[1] + table_mid.shape[1] + table_cold.shape[1]
    steps = 8

    def blocked(table):
        return pl.BlockSpec((table.shape[0] // steps, table.shape[1]), lambda i: (i, 0))

    return pl.pallas_call(
        functools.partial(gather_body, steps, cold_width),
        grid=(steps,),
        out_shape=sds((slots, width), BF16),
        in_specs=[
            pl.BlockSpec(serve_rows.shape, lambda i: (0, 0, 0)),
            blocked(table_hot),
            blocked(table_mid),
            blocked(table_cold),
        ],
        out_specs=pl.BlockSpec((slots, width), lambda i: (0, 0)),
        scratch_shapes=[
            pltpu.VMEM((8, slots), jnp.int32),
            pltpu.VMEM((slots, 8), jnp.int32),
            pltpu.VMEM((slots, width), F32),
        ],
        compiler_params=pltpu.CompilerParams(vmem_limit_bytes=24 * MIB),
        name="gather_rows",
    )(serve_rows, table_hot, table_mid, table_cold)


def count_body(slots, item_slot, item_block, by_item, by_slot, pad):
    fields, items = item_slot.shape[1], item_slot.shape[2]
    which = item_block[0] * slots + item_slot[0]
    pad[...] = jnp.zeros_like(pad)
    pad[0:fields, :] = which
    cols = pad[...].T
    for base in range(0, by_slot.shape[0], QB):
        rows = iota((QB, items), 0) + base
        total = jnp.zeros((QB, items), F32)
        for f in range(fields):
            total += ones_where(rows == which[f : f + 1, :])
        by_slot[base : base + QB, :] = total.astype(BF16)
        lanes = iota((items, QB), 1) + base
        total = jnp.zeros((items, QB), F32)
        for f in range(fields):
            total += ones_where(lanes == cols[:, f : f + 1])
        by_item[:, base : base + QB] = total.astype(BF16)


def tall(weight, times):
    return jnp.concatenate([weight] * times, axis=0)


def label_rows(label, base, jj):
    return label[0:1, jj * QB : (jj + 1) * QB] - base


def forward_body(peers, raw, counts, p_hot, p_mid, p_cold, t_in, t_out, *rest):
    queries, labels = rest[:peers], rest[peers : 2 * peers]
    pooled_o, resid_o, vec_o, stats_o, table = rest[2 * peers :]
    slots = raw.shape[0]
    w_hot, w_mid = p_hot.shape[0], p_mid.shape[0]
    w_cold = raw.shape[1] - w_hot - w_mid
    table[0:slots, :] = mm(raw[:, 0:w_hot], p_hot[...]).astype(BF16)
    table[slots : 2 * slots, :] = mm(raw[:, w_hot : w_hot + w_mid], p_mid[...]).astype(BF16)
    table[2 * slots :, :] = mm(
        raw[:, w_hot + w_mid :], tall(p_cold[...], w_cold // p_cold.shape[0])
    ).astype(BF16)
    items = counts.shape[0]
    for at in range(0, items, IB):
        rows = slice(at, at + IB)
        pooled = mm(counts[rows, :], table[...]).astype(BF16)
        pre = mm(pooled, t_in[...])
        hidden = (pre * jax.nn.sigmoid(pre)).astype(BF16)
        resid = pooled.astype(F32) + mm(hidden, t_out[...])
        inv = lax.rsqrt(jnp.mean(resid * resid, axis=1, keepdims=True) + NORM_EPS)
        pooled_o[rows, :] = pooled
        resid_o[rows, :] = resid
        vec_o[rows, :] = (resid * inv).astype(BF16)
    base = lax.axis_index("group") * items
    per = queries[0].shape[0] // QB
    for t in range(peers):
        for jj in range(per):
            s = mm(vec_o[...], queries[t][jj * QB : (jj + 1) * QB, :], NT) * LOGIT_SCALE
            top = jnp.max(s, axis=0, keepdims=True)
            total = jnp.sum(jnp.exp(s - top), axis=0, keepdims=True)
            hit = iota(s.shape, 0) == label_rows(labels[t], base, jj)
            picked = jnp.sum(jnp.where(hit, s, 0.0), axis=0, keepdims=True)
            j = t * per + jj
            stats_o[j : j + 1, 0:QB] = top
            stats_o[j : j + 1, QB : 2 * QB] = total
            stats_o[j : j + 1, 2 * QB :] = picked


class Plan:
    def __init__(self, groups, reps, width, inner, raw_width):
        self.groups, self.reps = groups, reps
        self.ky = groups // 2
        self.kx, self.kz = 2, reps // 2
        self.hr = inner // reps
        self.dr = width // reps
        self.b_in = width // LANES
        self.b_out = inner // LANES
        self.b_raw = raw_width // LANES
        rows = self.hr * self.b_in + self.dr * (self.b_out + self.b_raw)
        unit = 16 * self.ky
        units = -(-rows // (2 * unit))
        self.half = units * unit
        self.m1 = -(-units // 2) * 16
        self.m2 = units * 16 - self.m1
        self.rows = 2 * self.half
        self.used = rows
        self.p1 = reps * self.ky * self.m1
        self.p2 = reps * self.ky * self.m2


def backward_body(plan, peers, loss_dtype, *refs):
    stats, refs = refs[:peers], refs[peers:]
    queries, refs = refs[:peers], refs[peers:]
    labels, refs = refs[:peers], refs[peers:]
    vec, resid, pooled, by_slot, raw, p_hot, p_mid, p_cold, t_in, t_out = refs[:10]
    loss_o, grad_o, keep_o, send_o, back_o = refs[10:15]
    wide_s, low_s, hid_s, pre_s, pgrad_s, slot_s, chunk = refs[15:]
    items, width = vec.shape
    nq = queries[0].shape[0]
    per = nq // QB
    me_g, me_r = lax.axis_index("group"), lax.axis_index("rep")
    base = me_g * items
    for t in range(peers):
        for jj in range(per):
            rows = [(t ^ s) * per + jj for s in range(peers)]
            tops = [stats[s][rows[s] : rows[s] + 1, 0:QB] for s in range(peers)]
            totals = [stats[s][rows[s] : rows[s] + 1, QB : 2 * QB] for s in range(peers)]
            top = functools.reduce(jnp.maximum, tops)
            total = sum(tot * jnp.exp(m - top) for m, tot in zip(tops, totals))
            log_total = top + jnp.log(total)
            if t == 0:
                picked = sum(stats[s][rows[s] : rows[s] + 1, 2 * QB :] for s in range(peers))
                loss_o[0:1, jj * QB : (jj + 1) * QB] = log_total - picked
            s = mm(vec[...], queries[t][jj * QB : (jj + 1) * QB, :], NT) * LOGIT_SCALE
            hit = iota(s.shape, 0) == label_rows(labels[t], base, jj)
            grad = jnp.exp(s - log_total) - ones_where(hit)
            at = t * nq + jj * QB
            grad_o[:, at : at + QB] = grad.astype(BF16)
    for at in range(0, items, IB):
        rows = slice(at, at + IB)
        vgrad = mm(grad_o[rows, 0:nq], queries[0][...])
        for t in range(1, peers):
            vgrad += mm(grad_o[rows, t * nq : (t + 1) * nq], queries[t][...])
        vgrad = LOGIT_SCALE * vgrad
        res = resid[rows, :]
        inv = lax.rsqrt(jnp.mean(res * res, axis=1, keepdims=True) + NORM_EPS)
        dot_wide = jnp.sum(vgrad * res, axis=1, keepdims=True)
        wide = inv * vgrad - (inv * inv * inv / width * dot_wide) * res
        low = wide.astype(BF16)
        low_s[rows, :] = low
        pre = mm(pooled[rows, :], t_in[...])
        sig = jax.nn.sigmoid(pre)
        hid_s[rows, :] = (pre * sig).astype(BF16)
        pre_g = (mm(low, t_out[...], NT) * (sig * (1.0 + pre * (1.0 - sig)))).astype(BF16)
        pre_s[rows, :] = pre_g
        pgrad_s[rows, :] = (mm(pre_g, t_in[...], NT) + wide).astype(BF16)
    slots = raw.shape[0]
    w_hot, w_mid = p_hot.shape[0], p_mid.shape[0]
    w_cold = raw.shape[1] - w_hot - w_mid
    slot_s[...] = mm(by_slot[...], pgrad_s[...]).astype(BF16)
    back_o[:, 0:width] = slot_s[0:slots, :]
    back_o[:, width : width + w_mid] = mm(slot_s[slots : 2 * slots, :], p_mid[...], NT).astype(BF16)
    back_o[:, width + w_mid :] = mm(
        slot_s[2 * slots :, :], tall(p_cold[...], w_cold // p_cold.shape[0]), NT
    ).astype(BF16)

    g_in = mm(pooled[...], pre_s[...], TN).T
    hr, dr = plan.hr, plan.dr
    for r in range(plan.reps):
        for b in range(plan.b_in):
            chunk[r, b * hr : (b + 1) * hr, :] = g_in[
                r * hr : (r + 1) * hr, b * LANES : (b + 1) * LANES
            ].astype(BF16)
    at = hr * plan.b_in
    g_out = mm(low_s[...], hid_s[...], TN)
    parts = [(g_out, plan.b_out)]
    lane = 0
    for b, w in enumerate((w_hot, w_mid, w_cold)):
        parts.append(
            (mm(slot_s[b * slots : (b + 1) * slots, :], raw[:, lane : lane + w], TN), w // LANES)
        )
        lane += w
    for value, blocks in parts:
        for r in range(plan.reps):
            for b in range(blocks):
                chunk[r, at + b * dr : at + (b + 1) * dr, :] = value[
                    r * dr : (r + 1) * dr, b * LANES : (b + 1) * LANES
                ].astype(BF16)
        at += blocks * dr
    if plan.rows > plan.used:
        chunk[:, plan.used :, :] = jnp.zeros((plan.reps, plan.rows - plan.used, LANES), BF16)
    core, me_y = me_g & 1, lax.shift_right_logical(me_g, 1)
    for h, out in ((0, keep_o), (1, send_o)):
        start = (core ^ h) * plan.half
        for z in range(plan.kz):
            for x in range(plan.kx):
                r = me_r ^ (z * 2 + x)
                for y in range(plan.ky):
                    q = me_y ^ y
                    m = plan.m1
                    at = ((x * plan.ky + y) * plan.kz + z) * m
                    row = pl.multiple_of(start + q * m, 16)
                    out[at : at + m, :] = chunk[r, pl.ds(row, m), :]
                    m = plan.m2
                    if m:
                        at = plan.p1 + ((y * plan.kx + x) * plan.kz + z) * m
                        row = pl.multiple_of(start + plan.ky * plan.m1 + q * m, 16)
                        out[at : at + m, :] = chunk[r, pl.ds(row, m), :]


def query_grad_body(peers, vec, grad, keep_o, send_o):
    turned = vec[...].T
    nq = keep_o.shape[2]
    for t in range(peers):
        part = (LOGIT_SCALE * mm(turned, grad[:, t * nq : (t + 1) * nq])).astype(BF16)
        (send_o if t & 1 else keep_o)[t // 2] = part


def query_core_body(keep, got, own_o, *sends):
    own_o[...] = keep[0].astype(F32) + got[0].astype(F32)
    for y, out in enumerate(sends):
        out[...] = (keep[y + 1].astype(F32) + got[y + 1].astype(F32)).astype(BF16)


def query_final_body(own, *rest):
    got, out = rest[:-1], rest[-1]
    total = own[...]
    for part in got:
        total += part[...].astype(F32)
    out[...] = total.T


def cut_body(sources, cuts, *refs):
    n_in = len(refs) - len(cuts)
    for out, pieces in zip(refs[n_in:], cuts):
        for at, rows, terms in pieces:
            total = None
            for i, first in terms:
                part = refs[i][first : first + rows, :].astype(F32)
                total = part if total is None else total + part
            out[at : at + rows, :] = total.astype(out.dtype)


def cut(inputs, cuts, name):
    shapes = [sds((sum(p[1] for p in pieces), LANES), BF16) for pieces in cuts]
    return call(
        functools.partial(cut_body, None, cuts), shapes, inputs, vmem=16, name=name
    )


def final_body(plan, w_hot, w_mid, w_cold, cold_rows, *refs):
    pieces = refs[: plan.groups]
    o_in, o_out, o_hot, o_mid, o_cold, chunk = refs[plan.groups :]
    me_g = lax.axis_index("group")
    for t in range(plan.groups):
        h = (me_g & 1) ^ (t & 1)
        q = lax.shift_right_logical(me_g, 1) ^ (t >> 1)
        start = h * plan.half
        row = pl.multiple_of(start + q * plan.m1, 16)
        chunk[pl.ds(row, plan.m1), :] = pieces[t][0 : plan.m1, :].astype(F32)
        if plan.m2:
            row = pl.multiple_of(start + plan.ky * plan.m1 + q * plan.m2, 16)
            chunk[pl.ds(row, plan.m2), :] = pieces[t][plan.m1 :, :].astype(F32)
    hr, dr = plan.hr, plan.dr
    for b in range(plan.b_in):
        o_in[b * LANES : (b + 1) * LANES, :] = chunk[b * hr : (b + 1) * hr, :].T
    at = hr * plan.b_in
    for out, w in ((o_out, plan.b_out * LANES), (o_hot, w_hot), (o_mid, w_mid)):
        for b in range(w // LANES):
            out[b * LANES : (b + 1) * LANES, :] = chunk[at : at + dr, :].T
            at += dr
    total = jnp.zeros((cold_rows, dr), F32)
    for b in range(w_cold // LANES):
        turned = chunk[at : at + dr, :].T
        for k in range(LANES // cold_rows):
            total += turned[k * cold_rows : (k + 1) * cold_rows, :]
        at += dr
    o_cold[...] = total


def scatter_body(cold_width, served, back, p_hot, o_hot, o_mid, o_cold, pad, hot_s, cold_s):
    step = pl.program_id(0)
    width = p_hot.shape[1]
    w_mid = o_mid.shape[1]
    slots = back.shape[0]

    @pl.when(step == 0)
    def _():
        cols = columns_of(served, pad)
        hot_s[...] = mm(back[:, 0:width], p_hot[...], NT).astype(BF16)
        lines = back[:, width + w_mid :]
        mine = lax.div(iota(lines.shape, 1), cold_width) == (cols[:, 2:3] & 3)
        cold_s[...] = jnp.where(mine, lines.astype(F32), 0.0).astype(BF16)

    def put(out, row, values):
        block = out.shape[0]
        hit = iota((block, slots), 0) + step * block == row
        out[...] = mm(ones_where(hit).astype(BF16), values)

    rows = served[0]
    put(o_hot, rows[0:1, :], hot_s[...])
    put(o_mid, rows[1:2, :], back[:, width : width + w_mid])
    put(o_cold, lax.shift_right_logical(rows[2:3, :], 2), cold_s[...])


def scatter_rows(serve_rows, back, proj_hot, shapes, cold_width):
    slots = serve_rows.shape[2]
    steps = 8

    def blocked(shape):
        return pl.BlockSpec((shape[0] // steps, shape[1]), lambda i: (i, 0))

    return pl.pallas_call(
        functools.partial(scatter_body, cold_width),
        grid=(steps,),
        out_shape=[sds(shape, F32) for shape in shapes],
        in_specs=[
            pl.BlockSpec(serve_rows.shape, lambda i: (0, 0, 0)),
            pl.BlockSpec(back.shape, lambda i: (0, 0)),
            pl.BlockSpec(proj_hot.shape, lambda i: (0, 0)),
        ],
        out_specs=[blocked(shape) for shape in shapes],
        scratch_shapes=[
            pltpu.VMEM((8, slots), jnp.int32),
            pltpu.VMEM((slots, shapes[0][1]), BF16),
            pltpu.VMEM((slots, shapes[2][1]), BF16),
        ],
        compiler_params=pltpu.CompilerParams(vmem_limit_bytes=24 * MIB),
        name="scatter_rows",
    )(serve_rows, back, proj_hot)


def local(
    groups,
    reps,
    table_hot,
    table_mid,
    table_cold,
    proj_hot,
    proj_mid,
    proj_cold,
    tower_in,
    tower_out,
    queries,
    labels,
    item_slot,
    item_block,
    serve_rows,
):
    devices = groups * reps
    slots = serve_rows.shape[2]
    cold_width, width = proj_cold.shape
    inner = tower_in.shape[1]
    items = item_slot.shape[2]
    nq = queries.shape[0]
    w_hot, w_mid, w_cold = table_hot.shape[1], table_mid.shape[1], table_cold.shape[1]
    raw_width = w_hot + w_mid + w_cold
    plan = Plan(groups, reps, width, inner, raw_width)

    def across_group(value, t):
        pairs = [(g * reps + r, (g ^ t) * reps + r) for g in range(groups) for r in range(reps)]
        return lax.ppermute(value, AXES, pairs)

    def across_rep(value, t):
        pairs = [(g * reps + r, g * reps + (r ^ t)) for g in range(groups) for r in range(reps)]
        return lax.ppermute(value, AXES, pairs)

    def to_all(rows):
        each = rows.reshape(devices, slots // devices, rows.shape[1])
        return lax.all_to_all(each, AXES, 0, 0, tiled=True).reshape(rows.shape)

    raw = to_all(gather_rows(serve_rows, table_hot, table_mid, table_cold, cold_width))
    label_row = labels.reshape(1, nq)
    q_all = [queries] + [across_group(queries, t) for t in range(1, groups)]
    l_all = [label_row] + [across_group(label_row, t) for t in range(1, groups)]
    by_item, by_slot = call(
        functools.partial(count_body, slots),
        [sds((items, 3 * slots), BF16), sds((3 * slots, items), BF16)],
        [item_slot, item_block],
        scratch=[pltpu.VMEM((8, items), jnp.int32)],
        name="counts",
    )
    blocks = groups * nq // QB
    pooled, resid, vec, stats = call(
        functools.partial(forward_body, groups),
        [
            sds((items, width), BF16),
            sds((items, width), F32),
            sds((items, width), BF16),
            sds((blocks, 3 * QB), F32),
        ],
        [raw, by_item, proj_hot, proj_mid, proj_cold, tower_in, tower_out] + q_all + l_all,
        scratch=[pltpu.VMEM((3 * slots, width), BF16)],
        vmem=48,
        name="forward",
    )
    s_all = [stats] + [across_group(stats, t) for t in range(1, groups)]
    cut_rows = plan.p1 + plan.p2
    loss, grad, keep, send, back = call(
        functools.partial(backward_body, plan, groups, F32),
        [
            sds((1, nq), F32),
            sds((items, groups * nq), BF16),
            sds((cut_rows, LANES), BF16),
            sds((cut_rows, LANES), BF16),
            sds((slots, width + w_mid + w_cold), BF16),
        ],
        s_all
        + q_all
        + l_all
        + [vec, resid, pooled, by_slot, raw, proj_hot, proj_mid, proj_cold, tower_in, tower_out],
        scratch=[
            pltpu.VMEM((8, LANES), F32),
            pltpu.VMEM((items, width), BF16),
            pltpu.VMEM((items, inner), BF16),
            pltpu.VMEM((items, inner), BF16),
            pltpu.VMEM((items, width), BF16),
            pltpu.VMEM((3 * slots, width), BF16),
            pltpu.VMEM((reps, plan.rows, LANES), BF16),
        ],
        vmem=56,
        name="backward",
    )
    back = to_all(back)

    got = across_group(send, 1)
    ky, kx, kz, m1, m2 = plan.ky, plan.kx, plan.kz, plan.m1, plan.m2

    def both(first, rows):
        return [(0, first), (1, first)], rows

    n1, n2 = plan.p1 // kx, plan.p2 // ky
    cuts = []
    for x in range(kx):
        cuts.append([(0, n1, [(0, x * n1), (1, x * n1)])])
    for y in range(ky):
        cuts.append([(0, n2, [(0, plan.p1 + y * n2), (1, plan.p1 + y * n2)])])
    parts = cut([keep, got], cuts, "sum_core")
    a_keep, a_send = parts[0], parts[1:kx]
    b_keep, b_send = parts[kx], parts[kx + 1 :]
    a_got = [across_rep(v, x + 1) for x, v in enumerate(a_send)]
    b_got = [across_group(v, 2 * (y + 1)) for y, v in enumerate(b_send)]
    k1, k2 = n1 // ky, n2 // kx
    na, nb = 1 + len(a_got), 1 + len(b_got)
    cuts = [[(0, k1, [(i, y * k1) for i in range(na)])] for y in range(ky)]
    cuts += [[(0, k2, [(na + i, x * k2) for i in range(nb)])] for x in range(kx)]
    parts = cut([a_keep, *a_got, b_keep, *b_got], cuts, "sum_xy")
    a_keep, a_send = parts[0], parts[1:ky]
    b_keep, b_send = parts[ky], parts[ky + 1 :]
    a_got = [across_group(v, 2 * (y + 1)) for y, v in enumerate(a_send)]
    b_got = [across_rep(v, x + 1) for x, v in enumerate(b_send)]
    na, nb = 1 + len(a_got), 1 + len(b_got)
    cuts = [
        [
            (0, m1, [(i, z * m1) for i in range(na)]),
            (m1, m2, [(na + i, z * m2) for i in range(nb)]),
        ]
        for z in range(kz)
    ]
    parts = cut([a_keep, *a_got, b_keep, *b_got], cuts, "sum_yx")
    z_got = [across_rep(parts[z], 2 * z) for z in range(1, kz)]
    mine = cut(
        [parts[0], *z_got], [[(0, m1 + m2, [(i, 0) for i in range(kz)])]], "sum_z"
    )[0]
    pieces = [mine] + [across_group(mine, t) for t in range(1, groups)]
    g_in, g_out, g_hot, g_mid, g_cold = call(
        functools.partial(final_body, plan, w_hot, w_mid, w_cold, cold_width),
        [
            sds((width, inner // reps), F32),
            sds((inner, width // reps), F32),
            sds((w_hot, width // reps), F32),
            sds((w_mid, width // reps), F32),
            sds((cold_width, width // reps), F32),
        ],
        pieces,
        scratch=[pltpu.VMEM((plan.rows, LANES), F32)],
        vmem=16,
        name="weights_out",
    )

    q_keep, q_send = call(
        functools.partial(query_grad_body, groups),
        [sds((groups // 2, width, nq), BF16), sds((groups // 2, width, nq), BF16)],
        [vec, grad],
        vmem=32,
        name="query_grad",
    )
    q_got = across_group(q_send, 1)
    own, *q_sends = call(
        query_core_body,
        [sds((width, nq), F32)] + [sds((width, nq), BF16)] * (ky - 1),
        [q_keep, q_got],
        vmem=16,
        name="query_core",
    )
    q_parts = [across_group(v, 2 * (y + 1)) for y, v in enumerate(q_sends)]
    query_grad = call(
        query_final_body, sds((nq, width), F32), [own, *q_parts], vmem=16, name="query_out"
    )

    o_hot, o_mid, o_cold = scatter_rows(
        serve_rows, back, proj_hot, [table_hot.shape, table_mid.shape, table_cold.shape], cold_width
    )
    return (
        loss.reshape(nq),
        query_grad,
        o_hot,
        o_mid,
        o_cold,
        g_hot,
        g_mid,
        g_cold,
        g_in,
        g_out,
    )


def solution(mesh):
    split = P(AXES, None)
    deep = P(AXES, None, None)
    return jax.shard_map(
        functools.partial(local, mesh.shape["group"], mesh.shape["rep"]),
        mesh=mesh,
        in_specs=(split, split, split, P(), P(), P(), P(), P(), split, P(AXES), deep, deep, deep),
        out_specs=(P(AXES), split, split, split, split) + (P(None, "rep"),) * 5,
        check_vma=False,
    )
```

time: 319 us -> 118 us (0.37)
  waiting for transfers between devices: 101 us -> 32.7 us
  blocking collectives: 61.6 us -> 0 us
  other arithmetic: 48.3 us -> 0 us
  Pallas kernels: 0 us -> 37.1 us
  local copies, waits for them, and re-layouts: 43.6 us -> 14.3 us
  matrix products: 25.5 us -> 0 us
  between operations: 14.4 us -> 1.03 us
  starting transfers between devices: 22.8 us -> 31.9 us
    psum x1 -> x0, waiting for transfers between devices: 55.6 us -> none  [local(): lax.psum((grad_ph, grad_pm, grad_pc, grad_in_local, grad_out_local), ('gr...]
    psum x1 -> x0, blocking collectives: 40.7 us -> none  [local(): lax.psum((grad_ph, grad_pm, grad_pc, grad_in_local, grad_out_local), ('gr...]
    pallas_call x0 -> x13, Pallas kernels: none -> 37.1 us  [the longest x11 27.5 us: call(): pl.pallas_call(body, out_shape=out_shape, in_specs=[spec] * len(inputs),...]
    ppermute x0 -> x22, waiting for transfers between devices: none -> 32.7 us  [the longest x17 24.2 us: across_group(): return lax.ppermute(value, AXES, pairs)]
    scatter-add x4 -> x0, other arithmetic: 32.6 us -> none  [the longest x1 23 us: local(): jax.ops.segment_sum(stacked, slot_index.reshape(-1), num_segments=3 * slo...]
    dot_general x18 -> x0, matrix products: 25.5 us -> none  [the longest x6 7.8 us: contract(): lax.dot_general(left_rows, right_rows, (((0,), (0,)), ((), ())), preferre...]
    all_to_all x6 -> x2, waiting for transfers between devices: 24.8 us -> 0.01 us  [to_all(): return lax.all_to_all(each, AXES, 0, 0, tiled=True).reshape(rows.shape)]
    gather x5 -> x0, local copies, waits for them, and re-layouts: 23.3 us -> none  [the longest x1 16.6 us: local(): slot_table[slot_index].astype(jnp.float32)]
  transfers between devices with their start and end apart: 9 -> 24, of which waited for: 7 -> 8; matrix products, arithmetic and copies ran while one was open for 20% -> 0% of each run, Pallas kernels for 0% -> 10%
where the time goes in v1:
time: 118 us; the launch traced here: 117 us
  Pallas kernels  37.1 us (31%)
  waiting for transfers between devices  32.7 us (28%)
  starting transfers between devices  31.9 us (27%)
  local copies, waits for them, and re-layouts  14.3 us (12%)
    pallas_call x11, Pallas kernels, call(): pl.pallas_call(body, out_shape=out_shape, in_specs=[spec] * len(inputs),...  27.5 us
    ppermute x17, waiting for transfers between devices, across_group(): return lax.ppermute(value, AXES, pairs)  24.2 us
    unnamed x68, local copies, waits for them, and re-layouts  14.3 us
    all_to_all x2, starting transfers between devices, to_all(): return lax.all_to_all(each, AXES, 0, 0, tiled=True).reshape(rows.shape)  12.4 us
    ppermute x17, starting transfers between devices, across_group(): return lax.ppermute(value, AXES, pairs)  12.4 us
    ppermute x5, waiting for transfers between devices, across_rep(): return lax.ppermute(value, AXES, pairs)  8.5 us
    ppermute x5, starting transfers between devices, across_rep(): return lax.ppermute(value, AXES, pairs)  7.11 us
    pallas_call x1, Pallas kernels, scatter_rows(): pl.pallas_call(functools.partial(scatter_body, cold_width), grid=(steps,)...  5.19 us
  transfers between devices with their start and end apart: 24, of which 8 were waited for; matrix products, arithmetic and copies ran while one was open for 0% of the time, Pallas kernels for 10%

profile of v1, /device:TPU:0, one launch (start us, length us, event | category | flops | bytes accessed | tf_op | source)
XLA Modules:
  0.0 117.1 jit_solution(1179069602438392103)
XLA Ops:
  2.6 1.2 %copy-done.16 = bf16[4096,128]{1,0:T(8,128)(2,1)S(1)} copy-done((bf16[4096,128]{1,0:T(8,128)(2,1)S(1)}, bf16[4096,128]{1,0:T(8,128)(2,1)}, u32[]{:S(2)}) %copy-start.16) | copy-done | bytes 1048600
  3.8 1.2 %copy-done.17 = bf16[4096,128]{1,0:T(8,128)(2,1)S(1)} copy-done((bf16[4096,128]{1,0:T(8,128)(2,1)S(1)}, bf16[4096,128]{1,0:T(8,128)(2,1)}, u32[]{:S(2)}) %copy-start.17) | copy-done | bytes 1048600
  5.1 4.4 %gather_rows.1 = bf16[256,768]{1,0:T(8,128)(2,1)} custom-call(s32[1,3,256]{2,1,0:T(4,128)S(1)} %copy.23.served, bf16[1024,512]{1,0:T(8,128)(2,1)S(1)} %copy-done.15, bf16[4096,128]{1,0:T(8,128)(2,1)S(1)} %copy-done.16, bf16[4096,128]{1,0:T(8,128)(2,1)S(1)} %copy-done.17), custom_call_target="tpu_custom_call" | custom-call | tf_op jit(solution)/shard_map/gather_rows/pallas_call | solution.py:95
  9.5 7.3 %all-to-all-start = ((bf16[32,8,768]{2,1,0:T(8,128)(2,1)}), bf16[32,8,768]{2,1,0:T(8,128)(2,1)S(1)}, u32[]{:S(2)}, u32[]{:S(2)}) async-start(bf16[32,8,768]{2,1,0:T(8,128)(2,1)} %bitcast), calls=%async_computation | async-start | bytes 786432 | tf_op jit(solution)/shard_map/all_to_all | solution.py:461
  16.8 1.6 %collective-permute-start.2 = (bf16[512,256]{1,0:T(8,128)(2,1)S(1)}, bf16[512,256]{1,0:T(8,128)(2,1)S(1)}, u32[]{:S(2)}, u32[]{:S(2)}) collective-permute-start(bf16[512,256]{1,0:T(8,128)(2,1)S(1)} %copy-done.11), channel_id=1, source_target_pairs={{0,24},{1,25},{2,26},{3,27},{4,28},{5,29},{6,30},{7,31},{8,16},{9,... | collective-permute-start | bytes 786440 | tf_op jit(solution)/shard_map/ppermute | solution.py:453
  18.8 1.7 %collective-permute-start.5 = (s32[1,512]{1,0:T(1,128)S(1)}, s32[1,512]{1,0:T(1,128)S(1)}, u32[]{:S(2)}, u32[]{:S(2)}) collective-permute-start(s32[1,512]{1,0:T(1,128)S(1)} %bitcast.10), channel_id=1, source_target_pairs={{0,24},{1,25},{2,26},{3,27},{4,28},{5,29},{6,30},{7,31},{8,16},{9,... | collective-permute-start | bytes 6152 | tf_op jit(solution)/shard_map/ppermute | solution.py:453
  20.9 13.8 %collective-permute-done.5.rest_7_.refs_11_ = s32[1,512]{1,0:T(1,128)S(1)} collective-permute-done((s32[1,512]{1,0:T(1,128)S(1)}, s32[1,512]{1,0:T(1,128)S(1)}, u32[]{:S(2)}, u32[]{:S(2)}) %collective-permute-start.5) | collective-permute-done | bytes 2080 | tf_op jit(solution)/shard_map/ppermute | solution.py:453
  35.4 3.4 %counts.1 = (bf16[1024,768]{1,0:T(8,128)(2,1)S(1)}, bf16[768,1024]{1,0:T(8,128)(2,1)S(1)}) custom-call(s32[1,4,1024]{2,1,0:T(4,128)S(1)} %copy-done.23, s32[1,4,1024]{2,1,0:T(4,128)S(1)} %copy-done.24), custom_call_target="tpu_custom_call" | custom-call | tf_op jit(solution)/shard_map/counts/pallas_call | solution.py:39
  41.2 7.6 %forward.1 = (bf16[1024,256]{1,0:T(8,128)(2,1)S(1)}, f32[1024,256]{1,0:T(8,128)S(1)}, bf16[1024,256]{1,0:T(8,128)(2,1)S(1)}, f32[8,768]{1,0:T(8,128)S(1)}) custom-call(bf16[256,768]{1,0:T(8,128)(2,1)S(1)} %bitcast.6, bf16[1024,768]{1,0:T(8,128)(2,1)} %copy-done.8, bf16[512,256]{1,0:T(8,128)(2,1)S(1)} %copy-done.2, bf16[128,256]{1,0:T(8,128)(2,1)S(1)} %copy-done.20, ...), custom_call_target="tpu_custom_call" | custom-call | tf_op jit(solution)/shard_map/forward/pallas_call | solution.py:39
  53.3 1.5 %collective-permute-done.8.refs_3_ = f32[8,768]{1,0:T(8,128)S(1)} collective-permute-done((f32[8,768]{1,0:T(8,128)S(1)}, f32[8,768]{1,0:T(8,128)S(1)}, u32[]{:S(2)}, u32[]{:S(2)}) %collective-permute-start.8) | collective-permute-done | bytes 24608 | tf_op jit(solution)/shard_map/ppermute | solution.py:453
  56.5 12.9 %backward.1 = (f32[1,512]{1,0:T(1,128)}, bf16[1024,2048]{1,0:T(8,128)(2,1)}, bf16[2816,128]{1,0:T(8,128)(2,1)}, bf16[2816,128]{1,0:T(8,128)(2,1)}, bf16[256,512]{1,0:T(8,128)(2,1)}) custom-call(f32[8,768]{1,0:T(8,128)} %copy-done.22, f32[8,768]{1,0:T(8,128)} %copy-done.31, f32[8,768]{1,0:T(8,128)} %copy-done.30, f32[8,768]{1,0:T(8,128)} %copy-done.29, ...), custom_call_target="tpu_custom_call" | custom-call | tf_op jit(solution)/shard_map/backward/pallas_call | solution.py:39
  69.4 2.2 %copy-done = bf16[1024,2048]{1,0:T(8,128)(2,1)S(1)} copy-done((bf16[1024,2048]{1,0:T(8,128)(2,1)S(1)}, bf16[1024,2048]{1,0:T(8,128)(2,1)}, u32[]{:S(2)}) %copy-start) | copy-done | bytes 4194328
  71.6 1.3 %query_grad.1 = (bf16[2,256,512]{2,1,0:T(8,128)(2,1)S(1)}, bf16[2,256,512]{2,1,0:T(8,128)(2,1)S(1)}) custom-call(bf16[1024,256]{1,0:T(8,128)(2,1)S(1)} %copy-done.7, bf16[1024,2048]{1,0:T(8,128)(2,1)S(1)} %copy-done), custom_call_target="tpu_custom_call" | custom-call | tf_op jit(solution)/shard_map/query_grad/pallas_call | solution.py:39
  73.4 5.1 %all-to-all-start.1 = ((bf16[32,8,512]{2,1,0:T(8,128)(2,1)}), bf16[32,8,512]{2,1,0:T(8,128)(2,1)S(1)}, u32[]{:S(2)}, u32[]{:S(2)}) async-start(bf16[32,8,512]{2,1,0:T(8,128)(2,1)} %bitcast.14), calls=%async_computation.1 | async-start | bytes 524288 | tf_op jit(solution)/shard_map/all_to_all | solution.py:461
  78.8 1.8 %collective-permute-start.12 = (bf16[768,128]{1,0:T(8,128)(2,1)S(1)}, bf16[768,128]{1,0:T(8,128)(2,1)S(1)}, u32[]{:S(2)}, u32[]{:S(2)}) collective-permute-start(bf16[768,128]{1,0:T(8,128)(2,1)S(1)} %get-tuple-element.64), channel_id=1, source_target_pairs={{0,1},{1,0},{2,3},{3,2},{4,5},{5,4},{6,7},{7,6},{8,9},{9,8},{10,11... | collective-permute-start | bytes 589832 | tf_op jit(solution)/shard_map/ppermute | solution.py:457
  80.6 1.5 %collective-permute-start.13 = (bf16[640,128]{1,0:T(8,128)(2,1)S(1)}, bf16[640,128]{1,0:T(8,128)(2,1)S(1)}, u32[]{:S(2)}, u32[]{:S(2)}) collective-permute-start(bf16[640,128]{1,0:T(8,128)(2,1)S(1)} %get-tuple-element.66), channel_id=1, source_target_pairs={{0,16},{1,17},{2,18},{3,19},{4,20},{5,21},{6,22},{7,23},{8,24},{9,... | collective-permute-start | bytes 491528 | tf_op jit(solution)/shard_map/ppermute | solution.py:453
  82.8 6.3 %collective-permute-done.13.refs_3_ = bf16[640,128]{1,0:T(8,128)(2,1)S(1)} collective-permute-done((bf16[640,128]{1,0:T(8,128)(2,1)S(1)}, bf16[640,128]{1,0:T(8,128)(2,1)S(1)}, u32[]{:S(2)}, u32[]{:S(2)}) %collective-permute-start.13) | collective-permute-done | bytes 163872 | tf_op jit(solution)/shard_map/ppermute | solution.py:453
  91.2 3.6 %collective-permute-done.15.refs_3_ = bf16[320,128]{1,0:T(8,128)(2,1)S(1)} collective-permute-done((bf16[320,128]{1,0:T(8,128)(2,1)S(1)}, bf16[320,128]{1,0:T(8,128)(2,1)S(1)}, u32[]{:S(2)}, u32[]{:S(2)}) %collective-permute-start.15) | collective-permute-done | bytes 81952 | tf_op jit(solution)/shard_map/ppermute | solution.py:457
  94.8 1.6 %collective-permute-done.14.refs_1_ = bf16[384,128]{1,0:T(8,128)(2,1)S(1)} collective-permute-done((bf16[384,128]{1,0:T(8,128)(2,1)S(1)}, bf16[384,128]{1,0:T(8,128)(2,1)S(1)}, u32[]{:S(2)}, u32[]{:S(2)}) %collective-permute-start.14) | collective-permute-done | bytes 98336 | tf_op jit(solution)/shard_map/ppermute | solution.py:453
  96.4 1.5 %collective-permute-start.16 = (bf16[176,128]{1,0:T(8,128)(2,1)S(1)}, bf16[176,128]{1,0:T(8,128)(2,1)S(1)}, u32[]{:S(2)}, u32[]{:S(2)}) collective-permute-start(bf16[176,128]{1,0:T(8,128)(2,1)S(1)} %get-tuple-element.72), channel_id=1, source_target_pairs={{0,2},{1,3},{2,0},{3,1},{4,6},{5,7},{6,4},{7,5},{8,10},{9,11},{10,... | collective-permute-start | bytes 135176 | tf_op jit(solution)/shard_map/ppermute | solution.py:457
  97.9 2.0 %collective-permute-start.17 = (bf16[176,128]{1,0:T(8,128)(2,1)S(1)}, bf16[176,128]{1,0:T(8,128)(2,1)S(1)}, u32[]{:S(2)}, u32[]{:S(2)}) collective-permute-start(bf16[176,128]{1,0:T(8,128)(2,1)S(1)} %get-tuple-element.73), channel_id=1, source_target_pairs={{0,4},{1,5},{2,6},{3,7},{4,0},{5,1},{6,2},{7,3},{8,12},{9,13},{10,... | collective-permute-start | bytes 135176 | tf_op jit(solution)/shard_map/ppermute | solution.py:457
  100.9 2.5 %collective-permute-done.17.refs_2_ = bf16[176,128]{1,0:T(8,128)(2,1)S(1)} collective-permute-done((bf16[176,128]{1,0:T(8,128)(2,1)S(1)}, bf16[176,128]{1,0:T(8,128)(2,1)S(1)}, u32[]{:S(2)}, u32[]{:S(2)}) %collective-permute-start.17) | collective-permute-done | bytes 45088 | tf_op jit(solution)/shard_map/ppermute | solution.py:457
  103.3 2.4 %collective-permute-done.18.refs_3_ = bf16[176,128]{1,0:T(8,128)(2,1)S(1)} collective-permute-done((bf16[176,128]{1,0:T(8,128)(2,1)S(1)}, bf16[176,128]{1,0:T(8,128)(2,1)S(1)}, u32[]{:S(2)}, u32[]{:S(2)}) %collective-permute-start.18) | collective-permute-done | bytes 45088 | tf_op jit(solution)/shard_map/ppermute | solution.py:457
  107.7 5.2 %scatter_rows.1 = (f32[1024,512]{1,0:T(8,128)}, f32[4096,128]{1,0:T(8,128)}, f32[4096,128]{1,0:T(8,128)}) custom-call(s32[1,3,256]{2,1,0:T(4,128)S(1)} %copy.23.served, bf16[256,512]{1,0:T(8,128)(2,1)S(1)} %bitcast.8, bf16[512,256]{1,0:T(8,128)(2,1)S(1)} %copy-done.3), custom_call_target="tpu_custom_call" | custom-call | tf_op jit(solution)/shard_map/scatter_rows/pallas_call | solution.py:404
  (105 shorter events, 22.6 us)
Async XLA Ops:
  9.5 31.6 %all-to-all-start = ((bf16[32,8,768]{2,1,0:T(8,128)(2,1)}), bf16[32,8,768]{2,1,0:T(8,128)(2,1)S(1)}, u32[]{:S(2)}, u32[]{:S(2)}) async-start(bf16[32,8,768]{2,1,0:T(8,128)(2,1)} %bitcast), calls=%async_computation | async-start | bytes 786432 | tf_op jit(solution)/shard_map/all_to_all | solution.py:461
  16.8 24.2 %collective-permute-start.2 = (bf16[512,256]{1,0:T(8,128)(2,1)S(1)}, bf16[512,256]{1,0:T(8,128)(2,1)S(1)}, u32[]{:S(2)}, u32[]{:S(2)}) collective-permute-start(bf16[512,256]{1,0:T(8,128)(2,1)S(1)} %copy-done.11), channel_id=1, source_target_pairs={{0,24},{1,25},{2,26},{3,27},{4,28},{5,29},{6,30},{7,31},{8,16},{9,... | collective-permute-start | bytes 786440 | tf_op jit(solution)/shard_map/ppermute | solution.py:453
  18.4 22.7 %collective-permute-start.1 = (bf16[512,256]{1,0:T(8,128)(2,1)S(1)}, bf16[512,256]{1,0:T(8,128)(2,1)S(1)}, u32[]{:S(2)}, u32[]{:S(2)}) collective-permute-start(bf16[512,256]{1,0:T(8,128)(2,1)S(1)} %copy-done.11), channel_id=1, source_target_pairs={{0,16},{1,17},{2,18},{3,19},{4,20},{5,21},{6,22},{7,23},{8,24},{9,... | collective-permute-start | bytes 786440 | tf_op jit(solution)/shard_map/ppermute | solution.py:453
  18.8 22.3 %collective-permute-start = (bf16[512,256]{1,0:T(8,128)(2,1)S(1)}, bf16[512,256]{1,0:T(8,128)(2,1)S(1)}, u32[]{:S(2)}, u32[]{:S(2)}) collective-permute-start(bf16[512,256]{1,0:T(8,128)(2,1)S(1)} %copy-done.11), channel_id=1, source_target_pairs={{0,8},{1,9},{2,10},{3,11},{4,12},{5,13},{6,14},{7,15},{8,0},{9,1},... | collective-permute-start | bytes 786440 | tf_op jit(solution)/shard_map/ppermute | solution.py:453
  18.8 15.9 %collective-permute-start.5 = (s32[1,512]{1,0:T(1,128)S(1)}, s32[1,512]{1,0:T(1,128)S(1)}, u32[]{:S(2)}, u32[]{:S(2)}) collective-permute-start(s32[1,512]{1,0:T(1,128)S(1)} %bitcast.10), channel_id=1, source_target_pairs={{0,24},{1,25},{2,26},{3,27},{4,28},{5,29},{6,30},{7,31},{8,16},{9,... | collective-permute-start | bytes 6152 | tf_op jit(solution)/shard_map/ppermute | solution.py:453
  20.5 20.5 %collective-permute-start.4 = (s32[1,512]{1,0:T(1,128)S(1)}, s32[1,512]{1,0:T(1,128)S(1)}, u32[]{:S(2)}, u32[]{:S(2)}) collective-permute-start(s32[1,512]{1,0:T(1,128)S(1)} %bitcast.11), channel_id=1, source_target_pairs={{0,16},{1,17},{2,18},{3,19},{4,20},{5,21},{6,22},{7,23},{8,24},{9,... | collective-permute-start | bytes 6152 | tf_op jit(solution)/shard_map/ppermute | solution.py:453
  34.7 6.3 %collective-permute-start.3 = (s32[1,512]{1,0:T(1,128)S(1)}, s32[1,512]{1,0:T(1,128)S(1)}, u32[]{:S(2)}, u32[]{:S(2)}) collective-permute-start(s32[1,512]{1,0:T(1,128)S(1)} %bitcast.12), channel_id=1, source_target_pairs={{0,8},{1,9},{2,10},{3,11},{4,12},{5,13},{6,14},{7,15},{8,0},{9,1},... | collective-permute-start | bytes 6152 | tf_op jit(solution)/shard_map/ppermute | solution.py:453
  51.4 3.3 %collective-permute-start.8 = (f32[8,768]{1,0:T(8,128)S(1)}, f32[8,768]{1,0:T(8,128)S(1)}, u32[]{:S(2)}, u32[]{:S(2)}) collective-permute-start(f32[8,768]{1,0:T(8,128)S(1)} %get-tuple-element.46.refs_0_), channel_id=1, source_target_pairs={{0,24},{1,25},{2,26},{3,27},{4,28},{5,29},{6,30},{7,31},{8,16},{9,... | collective-permute-start | bytes 73736 | tf_op jit(solution)/shard_map/ppermute | solution.py:453
  52.0 3.8 %collective-permute-start.7 = (f32[8,768]{1,0:T(8,128)S(1)}, f32[8,768]{1,0:T(8,128)S(1)}, u32[]{:S(2)}, u32[]{:S(2)}) collective-permute-start(f32[8,768]{1,0:T(8,128)S(1)} %get-tuple-element.46.refs_0_), channel_id=1, source_target_pairs={{0,16},{1,17},{2,18},{3,19},{4,20},{5,21},{6,22},{7,23},{8,24},{9,... | collective-permute-start | bytes 73736 | tf_op jit(solution)/shard_map/ppermute | solution.py:453
  53.1 2.8 %collective-permute-start.6 = (f32[8,768]{1,0:T(8,128)S(1)}, f32[8,768]{1,0:T(8,128)S(1)}, u32[]{:S(2)}, u32[]{:S(2)}) collective-permute-start(f32[8,768]{1,0:T(8,128)S(1)} %get-tuple-element.46.refs_0_), channel_id=1, source_target_pairs={{0,8},{1,9},{2,10},{3,11},{4,12},{5,13},{6,14},{7,15},{8,0},{9,1},... | collective-permute-start | bytes 73736 | tf_op jit(solution)/shard_map/ppermute | solution.py:453
  69.3 9.2 %collective-permute-start.11 = (bf16[2816,128]{1,0:T(8,128)(2,1)}, bf16[2816,128]{1,0:T(8,128)(2,1)S(1)}, u32[]{:S(2)}, u32[]{:S(2)}) collective-permute-start(bf16[2816,128]{1,0:T(8,128)(2,1)} %get-tuple-element.62), channel_id=1, source_target_pairs={{0,8},{1,9},{2,10},{3,11},{4,12},{5,13},{6,14},{7,15},{8,0},{9,1},... | collective-permute-start | bytes 2162696 | tf_op jit(solution)/shard_map/ppermute | solution.py:453
  72.9 9.2 %collective-permute-start.9 = (bf16[2,256,512]{2,1,0:T(8,128)(2,1)S(1)}, bf16[2,256,512]{2,1,0:T(8,128)(2,1)S(1)}, u32[]{:S(2)}, u32[]{:S(2)}) collective-permute-start(bf16[2,256,512]{2,1,0:T(8,128)(2,1)S(1)} %get-tuple-element.54), channel_id=1, source_target_pairs={{0,8},{1,9},{2,10},{3,11},{4,12},{5,13},{6,14},{7,15},{8,0},{9,1},... | collective-permute-start | bytes 1572872 | tf_op jit(solution)/shard_map/ppermute | solution.py:453
  73.4 34.3 %all-to-all-start.1 = ((bf16[32,8,512]{2,1,0:T(8,128)(2,1)}), bf16[32,8,512]{2,1,0:T(8,128)(2,1)S(1)}, u32[]{:S(2)}, u32[]{:S(2)}) async-start(bf16[32,8,512]{2,1,0:T(8,128)(2,1)} %bitcast.14), calls=%async_computation.1 | async-start | bytes 524288 | tf_op jit(solution)/shard_map/all_to_all | solution.py:461
  78.8 10.3 %collective-permute-start.12 = (bf16[768,128]{1,0:T(8,128)(2,1)S(1)}, bf16[768,128]{1,0:T(8,128)(2,1)S(1)}, u32[]{:S(2)}, u32[]{:S(2)}) collective-permute-start(bf16[768,128]{1,0:T(8,128)(2,1)S(1)} %get-tuple-element.64), channel_id=1, source_target_pairs={{0,1},{1,0},{2,3},{3,2},{4,5},{5,4},{6,7},{7,6},{8,9},{9,8},{10,11... | collective-permute-start | bytes 589832 | tf_op jit(solution)/shard_map/ppermute | solution.py:457
  80.6 8.5 %collective-permute-start.13 = (bf16[640,128]{1,0:T(8,128)(2,1)S(1)}, bf16[640,128]{1,0:T(8,128)(2,1)S(1)}, u32[]{:S(2)}, u32[]{:S(2)}) collective-permute-start(bf16[640,128]{1,0:T(8,128)(2,1)S(1)} %get-tuple-element.66), channel_id=1, source_target_pairs={{0,16},{1,17},{2,18},{3,19},{4,20},{5,21},{6,22},{7,23},{8,24},{9,... | collective-permute-start | bytes 491528 | tf_op jit(solution)/shard_map/ppermute | solution.py:453
  82.2 30.7 %collective-permute-start.10 = (bf16[256,512]{1,0:T(8,128)(2,1)S(1)}, bf16[256,512]{1,0:T(8,128)(2,1)S(1)}, u32[]{:S(2)}, u32[]{:S(2)}) collective-permute-start(bf16[256,512]{1,0:T(8,128)(2,1)S(1)} %get-tuple-element.56), channel_id=1, source_target_pairs={{0,16},{1,17},{2,18},{3,19},{4,20},{5,21},{6,22},{7,23},{8,24},{9,... | collective-permute-start | bytes 786440 | tf_op jit(solution)/shard_map/ppermute | solution.py:453
  89.2 7.2 %collective-permute-start.14 = (bf16[384,128]{1,0:T(8,128)(2,1)S(1)}, bf16[384,128]{1,0:T(8,128)(2,1)S(1)}, u32[]{:S(2)}, u32[]{:S(2)}) collective-permute-start(bf16[384,128]{1,0:T(8,128)(2,1)S(1)} %get-tuple-element.68), channel_id=1, source_target_pairs={{0,16},{1,17},{2,18},{3,19},{4,20},{5,21},{6,22},{7,23},{8,24},{9,... | collective-permute-start | bytes 294920 | tf_op jit(solution)/shard_map/ppermute | solution.py:453
  90.3 4.4 %collective-permute-start.15 = (bf16[320,128]{1,0:T(8,128)(2,1)S(1)}, bf16[320,128]{1,0:T(8,128)(2,1)S(1)}, u32[]{:S(2)}, u32[]{:S(2)}) collective-permute-start(bf16[320,128]{1,0:T(8,128)(2,1)S(1)} %get-tuple-element.70), channel_id=1, source_target_pairs={{0,1},{1,0},{2,3},{3,2},{4,5},{5,4},{6,7},{7,6},{8,9},{9,8},{10,11... | collective-permute-start | bytes 245768 | tf_op jit(solution)/shard_map/ppermute | solution.py:457
  96.4 4.5 %collective-permute-start.16 = (bf16[176,128]{1,0:T(8,128)(2,1)S(1)}, bf16[176,128]{1,0:T(8,128)(2,1)S(1)}, u32[]{:S(2)}, u32[]{:S(2)}) collective-permute-start(bf16[176,128]{1,0:T(8,128)(2,1)S(1)} %get-tuple-element.72), channel_id=1, source_target_pairs={{0,2},{1,3},{2,0},{3,1},{4,6},{5,7},{6,4},{7,5},{8,10},{9,11},{10,... | collective-permute-start | bytes 135176 | tf_op jit(solution)/shard_map/ppermute | solution.py:457
  97.9 5.4 %collective-permute-start.17 = (bf16[176,128]{1,0:T(8,128)(2,1)S(1)}, bf16[176,128]{1,0:T(8,128)(2,1)S(1)}, u32[]{:S(2)}, u32[]{:S(2)}) collective-permute-start(bf16[176,128]{1,0:T(8,128)(2,1)S(1)} %get-tuple-element.73), channel_id=1, source_target_pairs={{0,4},{1,5},{2,6},{3,7},{4,0},{5,1},{6,2},{7,3},{8,12},{9,13},{10,... | collective-permute-start | bytes 135176 | tf_op jit(solution)/shard_map/ppermute | solution.py:457
  99.9 5.8 %collective-permute-start.18 = (bf16[176,128]{1,0:T(8,128)(2,1)S(1)}, bf16[176,128]{1,0:T(8,128)(2,1)S(1)}, u32[]{:S(2)}, u32[]{:S(2)}) collective-permute-start(bf16[176,128]{1,0:T(8,128)(2,1)S(1)} %get-tuple-element.74), channel_id=1, source_target_pairs={{0,6},{1,7},{2,4},{3,5},{4,2},{5,3},{6,0},{7,1},{8,14},{9,15},{10,... | collective-permute-start | bytes 135176 | tf_op jit(solution)/shard_map/ppermute | solution.py:457
  105.8 8.1 %collective-permute-start.21 = (bf16[176,128]{1,0:T(8,128)(2,1)S(1)}, bf16[176,128]{1,0:T(8,128)(2,1)S(1)}, u32[]{:S(2)}, u32[]{:S(2)}) collective-permute-start(bf16[176,128]{1,0:T(8,128)(2,1)S(1)} %sum_z.1.refs_0_), channel_id=1, source_target_pairs={{0,24},{1,25},{2,26},{3,27},{4,28},{5,29},{6,30},{7,31},{8,16},{9,... | collective-permute-start | bytes 135176 | tf_op jit(solution)/shard_map/ppermute | solution.py:453
  105.8 8.0 %collective-permute-start.20 = (bf16[176,128]{1,0:T(8,128)(2,1)S(1)}, bf16[176,128]{1,0:T(8,128)(2,1)S(1)}, u32[]{:S(2)}, u32[]{:S(2)}) collective-permute-start(bf16[176,128]{1,0:T(8,128)(2,1)S(1)} %sum_z.1.refs_0_), channel_id=1, source_target_pairs={{0,16},{1,17},{2,18},{3,19},{4,20},{5,21},{6,22},{7,23},{8,24},{9,... | collective-permute-start | bytes 135176 | tf_op jit(solution)/shard_map/ppermute | solution.py:453
  106.8 7.1 %collective-permute-start.19 = (bf16[176,128]{1,0:T(8,128)(2,1)S(1)}, bf16[176,128]{1,0:T(8,128)(2,1)S(1)}, u32[]{:S(2)}, u32[]{:S(2)}) collective-permute-start(bf16[176,128]{1,0:T(8,128)(2,1)S(1)} %sum_z.1.refs_0_), channel_id=1, source_target_pairs={{0,8},{1,9},{2,10},{3,11},{4,12},{5,13},{6,14},{7,15},{8,0},{9,1},... | collective-permute-start | bytes 135176 | tf_op jit(solution)/shard_map/ppermute | solution.py:453
  (32 other events, 399.0 us)

commit v2 on v1

v2 whole, which is shorter than its diff:
```python
import functools

import jax
import jax.numpy as jnp
from jax import lax
from jax.experimental import pallas as pl
from jax.experimental.pallas import tpu as pltpu
from jax.sharding import PartitionSpec as P


NORM_EPS = 1e-06
LOGIT_SCALE = 0.2
LOG2_E = 1.4426950408889634
AXES = ("group", "rep")
LANES = 128
QB = 256
IB = 256
MIB = 1 << 20
F32 = jnp.float32
BF16 = jnp.bfloat16

NN = (((1,), (0,)), ((), ()))
NT = (((1,), (1,)), ((), ()))
TN = (((0,), (0,)), ((), ()))


def mm(left, right, dims=NN):
    return lax.dot_general(left, right, dims, preferred_element_type=F32)


def ones_where(mask):
    return jnp.where(mask, jnp.float32(1), jnp.float32(0))


def iota(shape, dim):
    return lax.broadcasted_iota(jnp.int32, shape, dim)


def call(body, out_shape, inputs, far=(), scratch=(), vmem=40):
    spec = pl.BlockSpec(memory_space=pltpu.VMEM)
    return pl.pallas_call(
        body,
        out_shape=out_shape,
        in_specs=[spec] * len(inputs) + [pl.BlockSpec(memory_space=pltpu.HBM)] * len(far),
        out_specs=jax.tree.map(lambda _: spec, out_shape),
        scratch_shapes=list(scratch),
        compiler_params=pltpu.CompilerParams(vmem_limit_bytes=vmem * MIB),
    )(*inputs, *far)


def sds(shape, dtype):
    return jax.ShapeDtypeStruct(shape, dtype)


def columns_of(served, pad_ref):
    pad_ref[...] = jnp.zeros_like(pad_ref)
    for k in range(served.shape[0]):
        pad_ref[k : k + 1, :] = served[k]
    return pad_ref[...].T


def parts_of(shape, lanes):
    return max(1, lanes // shape[1])


def split_row(row, part):
    return lax.div(row, part), lax.rem(row, part)


def gather_body(cold_width, served, hot, mid, cold, out, pad, v_hot, v_mid, v_cold, sems):
    copies = []
    sem = 0
    for table, wide in ((hot, v_hot), (mid, v_mid), (cold, v_cold)):
        part, w = wide.shape[0], table.shape[1]
        group = []
        for k in range(wide.shape[1] // w):
            copy = pltpu.make_async_copy(
                table.at[pl.ds(k * part, part), :],
                wide.at[:, pl.ds(k * w, w)],
                sems.at[sem],
            )
            sem += 1
            copy.start()
            group.append(copy)
        copies.append(group)
    idx = columns_of(served, pad)
    slots = out.shape[0]

    def pick(group, wide, row, w):
        part = wide.shape[0]
        which, low = split_row(row, part)
        hit = ones_where(iota((slots, part), 1) == low).astype(BF16)
        for copy in group:
            copy.wait()
        found = mm(hit, wide[...])
        value = found[:, 0:w]
        for k in range(1, wide.shape[1] // w):
            value = jnp.where(which == k, found[:, k * w : (k + 1) * w], value)
        return value

    w_hot, w_mid, w_cold = hot.shape[1], mid.shape[1], cold.shape[1]
    out[:, 0:w_hot] = pick(copies[0], v_hot, idx[:, 0:1], w_hot).astype(BF16)
    out[:, w_hot : w_hot + w_mid] = pick(copies[1], v_mid, idx[:, 1:2], w_mid).astype(BF16)
    row = idx[:, 2:3]
    lines = pick(copies[2], v_cold, lax.shift_right_logical(row, 2), w_cold)
    mine = lax.div(iota(lines.shape, 1), cold_width) == (row & 3)
    out[:, w_hot + w_mid :] = jnp.where(mine, lines, 0.0).astype(BF16)


def gather_rows(served, table_hot, table_mid, table_cold, cold_width):
    slots = served.shape[2]
    tables = (table_hot, table_mid, table_cold)
    width = sum(table.shape[1] for table in tables)
    lanes = max(table.shape[1] for table in tables)
    parts = [parts_of(table.shape, lanes) for table in tables]
    hbm = pl.BlockSpec(memory_space=pltpu.HBM)
    vmem = pl.BlockSpec(memory_space=pltpu.VMEM)
    return pl.pallas_call(
        functools.partial(gather_body, cold_width),
        out_shape=sds((slots, width), BF16),
        in_specs=[vmem, hbm, hbm, hbm],
        out_specs=vmem,
        scratch_shapes=[pltpu.VMEM((8, slots), jnp.int32)]
        + [
            pltpu.VMEM((t.shape[0] // p, t.shape[1] * p), BF16) for t, p in zip(tables, parts)
        ]
        + [pltpu.SemaphoreType.DMA((sum(parts),))],
        compiler_params=pltpu.CompilerParams(vmem_limit_bytes=60 * MIB),
        name="gather_rows",
    )(served, *tables)


def slot_of(slots, item_slot, item_block):
    return item_block[0] * slots + item_slot[0]


def count_body(slots, item_slot, item_block, by_item, pad):
    fields, items = item_slot.shape[1], item_slot.shape[2]
    pad[...] = jnp.zeros_like(pad)
    pad[0:fields, :] = slot_of(slots, item_slot, item_block)
    cols = pad[...].T
    for base in range(0, by_item.shape[1], QB):
        lanes = iota((items, QB), 1) + base
        total = jnp.zeros((items, QB), F32)
        for f in range(fields):
            total += ones_where(lanes == cols[:, f : f + 1])
        by_item[:, base : base + QB] = total.astype(BF16)


def count_slots(which, by_slot):
    for base in range(0, by_slot.shape[0], QB):
        rows = iota((QB, which.shape[1]), 0) + base
        total = jnp.zeros((QB, which.shape[1]), F32)
        for f in range(which.shape[0]):
            total += ones_where(rows == which[f : f + 1, :])
        by_slot[base : base + QB, :] = total.astype(BF16)


def tall(weight, times):
    return jnp.concatenate([weight] * times, axis=0)


def label_rows(label, base, jj):
    return label[0:1, jj * QB : (jj + 1) * QB] - base


def sigmoid(value):
    return 0.5 + 0.5 * jnp.tanh(0.5 * value)


def forward_body(peers, raw, p_hot, p_mid, p_cold, *rest):
    labels, far = rest[:peers], rest[peers : 2 * peers + 3]
    pooled_o, resid_o, vec_o, stats_o, exp_o, table = rest[2 * peers + 3 : 2 * peers + 9]
    near, sems = rest[2 * peers + 9 : -1], rest[-1]
    copies = [
        pltpu.make_async_copy(source, target, sems.at[k])
        for k, (source, target) in enumerate(zip(far, near))
    ]
    for copy in copies:
        copy.start()
    counts, t_in, t_out = near[:3]
    queries = near[3:]
    slots = raw.shape[0]
    w_hot, w_mid = p_hot.shape[0], p_mid.shape[0]
    w_cold = raw.shape[1] - w_hot - w_mid
    table[0:slots, :] = mm(raw[:, 0:w_hot], p_hot[...]).astype(BF16)
    table[slots : 2 * slots, :] = mm(raw[:, w_hot : w_hot + w_mid], p_mid[...]).astype(BF16)
    table[2 * slots :, :] = mm(
        raw[:, w_hot + w_mid :], tall(p_cold[...], w_cold // p_cold.shape[0])
    ).astype(BF16)
    items = counts.shape[0]
    for copy in copies[:3]:
        copy.wait()
    for at in range(0, items, IB):
        rows = slice(at, at + IB)
        pooled = mm(counts[rows, :], table[...]).astype(BF16)
        pre = mm(pooled, t_in[...])
        hidden = (pre * sigmoid(pre)).astype(BF16)
        resid = pooled.astype(F32) + mm(hidden, t_out[...])
        inv = lax.rsqrt(jnp.mean(resid * resid, axis=1, keepdims=True) + NORM_EPS)
        pooled_o[rows, :] = pooled
        resid_o[rows, :] = resid
        vec_o[rows, :] = (resid * inv).astype(BF16)
    base = lax.axis_index("group") * items
    per = queries[0].shape[0] // QB
    for t in range(peers):
        copies[3 + t].wait()
        for jj in range(per):
            s = mm(vec_o[...], queries[t][jj * QB : (jj + 1) * QB, :], NT)
            top = jnp.max(s, axis=0, keepdims=True)
            grown = jnp.exp2((s - top) * (LOGIT_SCALE * LOG2_E))
            total = jnp.sum(grown, axis=0, keepdims=True)
            hit = iota(s.shape, 0) == label_rows(labels[t], base, jj)
            picked = jnp.sum(jnp.where(hit, s, 0.0), axis=0, keepdims=True)
            j = t * per + jj
            exp_o[:, j * QB : (j + 1) * QB] = grown
            stats_o[j : j + 1, 0:QB] = LOGIT_SCALE * top
            stats_o[j : j + 1, QB : 2 * QB] = total
            stats_o[j : j + 1, 2 * QB :] = LOGIT_SCALE * picked


def slope_body(slots, item_slot, item_block, pooled, t_in, hidden_o, slope_o, by_slot):
    count_slots(slot_of(slots, item_slot, item_block), by_slot)
    for at in range(0, pooled.shape[0], IB):
        rows = slice(at, at + IB)
        pre = mm(pooled[rows, :], t_in[...])
        sig = sigmoid(pre)
        hidden_o[rows, :] = (pre * sig).astype(BF16)
        slope_o[rows, :] = sig * (1.0 + pre * (1.0 - sig))


class Plan:
    def __init__(self, groups, reps, width, inner, raw_width):
        self.groups, self.reps = groups, reps
        self.ky = groups // 2
        self.kx, self.kz = 2, reps // 2
        self.hr = inner // reps
        self.dr = width // reps
        self.b_in = width // LANES
        self.b_out = inner // LANES
        self.b_raw = raw_width // LANES
        rows = self.hr * self.b_in + self.dr * (self.b_out + self.b_raw)
        unit = 16 * self.ky
        units = -(-rows // (2 * unit))
        self.half = units * unit
        self.m1 = -(-units // 2) * 16
        self.m2 = units * 16 - self.m1
        self.rows = 2 * self.half
        self.used = rows
        self.p1 = reps * self.ky * self.m1
        self.p2 = reps * self.ky * self.m2


def backward_body(plan, peers, *refs):
    stats, refs = refs[:peers], refs[peers:]
    queries, refs = refs[:peers], refs[peers:]
    labels, refs = refs[:peers], refs[peers:]
    grown, hidden, slope, resid, pooled, by_slot, raw, p_hot, p_mid, p_cold, t_in, t_out = refs[:12]
    loss_o, grad_o, keep_o, send_o, back_o = refs[12:17]
    low_s, pre_s, pgrad_s, slot_s, chunk = refs[17:]
    items, width = pooled.shape
    nq = queries[0].shape[0]
    per = nq // QB
    me_g, me_r = lax.axis_index("group"), lax.axis_index("rep")
    base = me_g * items
    for t in range(peers):
        for jj in range(per):
            rows = [(t ^ s) * per + jj for s in range(peers)]
            tops = [stats[s][rows[s] : rows[s] + 1, 0:QB] for s in range(peers)]
            totals = [stats[s][rows[s] : rows[s] + 1, QB : 2 * QB] for s in range(peers)]
            top = functools.reduce(jnp.maximum, tops)
            total = sum(tot * jnp.exp(m - top) for m, tot in zip(tops, totals))
            log_total = top + jnp.log(total)
            if t == 0:
                picked = sum(stats[s][rows[s] : rows[s] + 1, 2 * QB :] for s in range(peers))
                loss_o[0:1, jj * QB : (jj + 1) * QB] = log_total - picked
            at = t * nq + jj * QB
            share = grown[:, at : at + QB] * jnp.exp(tops[0] - log_total)
            hit = iota(share.shape, 0) == label_rows(labels[t], base, jj)
            grad_o[:, at : at + QB] = (share - ones_where(hit)).astype(BF16)
    for at in range(0, items, IB):
        rows = slice(at, at + IB)
        vgrad = mm(grad_o[rows, 0:nq], queries[0][...])
        for t in range(1, peers):
            vgrad += mm(grad_o[rows, t * nq : (t + 1) * nq], queries[t][...])
        vgrad = LOGIT_SCALE * vgrad
        res = resid[rows, :]
        inv = lax.rsqrt(jnp.mean(res * res, axis=1, keepdims=True) + NORM_EPS)
        dot_wide = jnp.sum(vgrad * res, axis=1, keepdims=True)
        wide = inv * vgrad - (inv * inv * inv / width * dot_wide) * res
        low = wide.astype(BF16)
        low_s[rows, :] = low
        pre_g = (mm(low, t_out[...], NT) * slope[rows, :]).astype(BF16)
        pre_s[rows, :] = pre_g
        pgrad_s[rows, :] = (mm(pre_g, t_in[...], NT) + wide).astype(BF16)
    slots = raw.shape[0]
    w_hot, w_mid = p_hot.shape[0], p_mid.shape[0]
    w_cold = raw.shape[1] - w_hot - w_mid
    slot_s[...] = mm(by_slot[...], pgrad_s[...]).astype(BF16)
    back_o[:, 0:width] = slot_s[0:slots, :]
    back_o[:, width : width + w_mid] = mm(slot_s[slots : 2 * slots, :], p_mid[...], NT).astype(BF16)
    back_o[:, width + w_mid :] = mm(
        slot_s[2 * slots :, :], tall(p_cold[...], w_cold // p_cold.shape[0]), NT
    ).astype(BF16)

    g_in = mm(pooled[...], pre_s[...], TN).T
    hr, dr = plan.hr, plan.dr
    for r in range(plan.reps):
        for b in range(plan.b_in):
            chunk[r, b * hr : (b + 1) * hr, :] = g_in[
                r * hr : (r + 1) * hr, b * LANES : (b + 1) * LANES
            ].astype(BF16)
    at = hr * plan.b_in
    g_out = mm(low_s[...], hidden[...], TN)
    parts = [(g_out, plan.b_out)]
    lane = 0
    for b, w in enumerate((w_hot, w_mid, w_cold)):
        parts.append(
            (mm(slot_s[b * slots : (b + 1) * slots, :], raw[:, lane : lane + w], TN), w // LANES)
        )
        lane += w
    for value, blocks in parts:
        for r in range(plan.reps):
            for b in range(blocks):
                chunk[r, at + b * dr : at + (b + 1) * dr, :] = value[
                    r * dr : (r + 1) * dr, b * LANES : (b + 1) * LANES
                ].astype(BF16)
        at += blocks * dr
    if plan.rows > plan.used:
        chunk[:, plan.used :, :] = jnp.zeros((plan.reps, plan.rows - plan.used, LANES), BF16)
    core, me_y = me_g & 1, lax.shift_right_logical(me_g, 1)
    for h, out in ((0, keep_o), (1, send_o)):
        start = (core ^ h) * plan.half
        for z in range(plan.kz):
            for x in range(plan.kx):
                r = me_r ^ (z * 2 + x)
                for y in range(plan.ky):
                    q = me_y ^ y
                    m = plan.m1
                    at = ((x * plan.ky + y) * plan.kz + z) * m
                    row = pl.multiple_of(start + q * m, 16)
                    out[at : at + m, :] = chunk[r, pl.ds(row, m), :]
                    m = plan.m2
                    if m:
                        at = plan.p1 + ((y * plan.kx + x) * plan.kz + z) * m
                        row = pl.multiple_of(start + plan.ky * plan.m1 + q * m, 16)
                        out[at : at + m, :] = chunk[r, pl.ds(row, m), :]


def query_grad_body(peers, vec, grad, keep_o, send_o):
    turned = vec[...].T
    nq = keep_o.shape[2]
    for t in range(peers):
        part = (LOGIT_SCALE * mm(turned, grad[:, t * nq : (t + 1) * nq])).astype(BF16)
        (send_o if t & 1 else keep_o)[t // 2] = part


def query_core_body(keep, got, own_o, *sends):
    own_o[...] = keep[0].astype(F32) + got[0].astype(F32)
    for y, out in enumerate(sends):
        out[...] = (keep[y + 1].astype(F32) + got[y + 1].astype(F32)).astype(BF16)


def query_final_body(own, *rest):
    got, out = rest[:-1], rest[-1]
    total = own[...]
    for part in got:
        total += part[...].astype(F32)
    out[...] = total.T


def cut_body(cuts, *refs):
    n_in = len(refs) - len(cuts)
    for out, pieces in zip(refs[n_in:], cuts):
        for at, rows, terms in pieces:
            total = None
            for i, first in terms:
                part = refs[i][first : first + rows, :].astype(F32)
                total = part if total is None else total + part
            out[at : at + rows, :] = total.astype(out.dtype)


def cut(inputs, cuts):
    shapes = [sds((sum(p[1] for p in pieces), LANES), BF16) for pieces in cuts]
    return call(functools.partial(cut_body, cuts), shapes, inputs, vmem=8)


def final_body(plan, w_hot, w_mid, w_cold, cold_rows, *refs):
    pieces = refs[: plan.groups]
    o_in, o_out, o_hot, o_mid, o_cold, chunk = refs[plan.groups :]
    me_g = lax.axis_index("group")
    for t in range(plan.groups):
        h = (me_g & 1) ^ (t & 1)
        q = lax.shift_right_logical(me_g, 1) ^ (t >> 1)
        start = h * plan.half
        row = pl.multiple_of(start + q * plan.m1, 16)
        chunk[pl.ds(row, plan.m1), :] = pieces[t][0 : plan.m1, :].astype(F32)
        if plan.m2:
            row = pl.multiple_of(start + plan.ky * plan.m1 + q * plan.m2, 16)
            chunk[pl.ds(row, plan.m2), :] = pieces[t][plan.m1 :, :].astype(F32)
    hr, dr = plan.hr, plan.dr
    for b in range(plan.b_in):
        o_in[b * LANES : (b + 1) * LANES, :] = chunk[b * hr : (b + 1) * hr, :].T
    at = hr * plan.b_in
    for out, w in ((o_out, plan.b_out * LANES), (o_hot, w_hot), (o_mid, w_mid)):
        for b in range(w // LANES):
            out[:, b * LANES : (b + 1) * LANES] = chunk[at : at + dr, :]
            at += dr
    total = jnp.zeros((cold_rows, dr), F32)
    for _ in range(w_cold // LANES):
        turned = chunk[at : at + dr, :].T
        for k in range(LANES // cold_rows):
            total += turned[k * cold_rows : (k + 1) * cold_rows, :]
        at += dr
    o_cold[...] = total


def scatter_body(cold_width, served, back, p_hot, o_hot, o_mid, o_cold, pad, s_hot, s_mid, s_cold):
    step = pl.program_id(0)
    steps = pl.num_programs(0)
    width = p_hot.shape[1]
    slots = back.shape[0]
    w_mid = o_mid.shape[2]

    @pl.when(step == 0)
    def _():
        cols = columns_of(served, pad)
        s_hot[...] = mm(back[:, 0:width], p_hot[...], NT).astype(BF16)

        def widen(wide, row, part, values):
            w = values.shape[1]
            which = split_row(row, part)[0]
            for k in range(wide.shape[1] // w):
                wide[:, k * w : (k + 1) * w] = jnp.where(which == k, values, 0.0).astype(BF16)

        mids = back[:, width : width + w_mid].astype(F32)
        widen(s_mid, cols[:, 1:2], o_mid.shape[1] * steps, mids)
        lines = back[:, width + w_mid :].astype(F32)
        mine = lax.div(iota(lines.shape, 1), cold_width) == (cols[:, 2:3] & 3)
        row = lax.shift_right_logical(cols[:, 2:3], 2)
        widen(s_cold, row, o_cold.shape[1] * steps, jnp.where(mine, lines, 0.0))

    def put(out, row, wide):
        block, w = out.shape[1], out.shape[2]
        low = split_row(row, block * steps)[1]
        hit = ones_where(iota((block, slots), 0) + step * block == low).astype(BF16)
        found = mm(hit, wide[...])
        for k in range(out.shape[0]):
            out[k] = found[:, k * w : (k + 1) * w]

    put(o_hot, served[0], s_hot)
    put(o_mid, served[1], s_mid)
    put(o_cold, lax.shift_right_logical(served[2], 2), s_cold)


def scatter_rows(served, back, proj_hot, shapes, cold_width):
    slots = served.shape[2]
    steps = 8
    lanes = max(shape[1] for shape in shapes)
    wide = [(parts_of(shape, lanes), shape) for shape in shapes]
    outs = [(p, shape[0] // p, shape[1]) for p, shape in wide]
    found = pl.pallas_call(
        functools.partial(scatter_body, cold_width),
        grid=(steps,),
        out_shape=[sds(shape, F32) for shape in outs],
        in_specs=[
            pl.BlockSpec(served.shape, lambda i: (0, 0, 0)),
            pl.BlockSpec(back.shape, lambda i: (0, 0)),
            pl.BlockSpec(proj_hot.shape, lambda i: (0, 0)),
        ],
        out_specs=[
            pl.BlockSpec((p, rows // steps, w), lambda i: (0, i, 0)) for p, rows, w in outs
        ],
        scratch_shapes=[pltpu.VMEM((8, slots), jnp.int32)]
        + [pltpu.VMEM((slots, p * w), BF16) for p, _, w in outs],
        compiler_params=pltpu.CompilerParams(vmem_limit_bytes=12 * MIB),
        name="scatter_rows",
    )(served, back, proj_hot)
    return [value.reshape(shape) for value, shape in zip(found, shapes)]


def local(
    groups,
    reps,
    table_hot,
    table_mid,
    table_cold,
    proj_hot,
    proj_mid,
    proj_cold,
    tower_in,
    tower_out,
    queries,
    labels,
    item_slot,
    item_block,
    serve_rows,
):
    devices = groups * reps
    slots = serve_rows.shape[2]
    cold_width, width = proj_cold.shape
    inner = tower_in.shape[1]
    items = item_slot.shape[2]
    nq = queries.shape[0]
    w_hot, w_mid, w_cold = table_hot.shape[1], table_mid.shape[1], table_cold.shape[1]
    raw_width = w_hot + w_mid + w_cold
    plan = Plan(groups, reps, width, inner, raw_width)

    def across_group(value, t):
        pairs = [(g * reps + r, (g ^ t) * reps + r) for g in range(groups) for r in range(reps)]
        return lax.ppermute(value, AXES, pairs)

    def across_rep(value, t):
        pairs = [(g * reps + r, g * reps + (r ^ t)) for g in range(groups) for r in range(reps)]
        return lax.ppermute(value, AXES, pairs)

    def to_all(rows):
        each = rows.reshape(devices, slots // devices, rows.shape[1])
        return lax.all_to_all(each, AXES, 0, 0, tiled=True).reshape(rows.shape)

    def to_group(value):
        found = {0: value}
        for t in range(2, groups, 2):
            found[t] = across_group(value, t)
        for t in range(0, groups, 2):
            found[t + 1] = across_group(found[t], 1)
        return [found[t] for t in range(groups)]

    served = jnp.transpose(serve_rows, (1, 0, 2))
    q_all = to_group(queries)
    rows = gather_rows(served, table_hot, table_mid, table_cold, cold_width)
    raw = to_all(rows)
    l_all = to_group(labels.reshape(1, nq))
    by_item = call(
        functools.partial(count_body, slots),
        sds((items, 3 * slots), BF16),
        [item_slot, item_block],
        scratch=[pltpu.VMEM((8, items), jnp.int32)],
        vmem=60,
    )
    blocks = groups * nq // QB
    far = [by_item, tower_in, tower_out] + q_all
    pooled, resid, vec, stats, grown = call(
        functools.partial(forward_body, groups),
        [
            sds((items, width), BF16),
            sds((items, width), F32),
            sds((items, width), BF16),
            sds((blocks, 3 * QB), F32),
            sds((items, groups * nq), F32),
        ],
        [raw, proj_hot, proj_mid, proj_cold] + l_all,
        far,
        scratch=[pltpu.VMEM((3 * slots, width), BF16)]
        + [pltpu.VMEM(value.shape, value.dtype) for value in far]
        + [pltpu.SemaphoreType.DMA((len(far),))],
        vmem=26 + 2 * groups,
    )
    s_all = [stats]
    for t in range(1, groups):
        s_all.append(across_group(stats, t))
    hidden, slope, by_slot = call(
        functools.partial(slope_body, slots),
        [sds((items, inner), BF16), sds((items, inner), F32), sds((3 * slots, items), BF16)],
        [item_slot, item_block, pooled, tower_in],
        vmem=12,
    )
    cut_rows = plan.p1 + plan.p2
    loss, grad, keep, send, back = call(
        functools.partial(backward_body, plan, groups),
        [
            sds((1, nq), F32),
            sds((items, groups * nq), BF16),
            sds((cut_rows, LANES), BF16),
            sds((cut_rows, LANES), BF16),
            sds((slots, width + w_mid + w_cold), BF16),
        ],
        s_all
        + q_all
        + l_all
        + [grown, hidden, slope, resid, pooled, by_slot, raw]
        + [proj_hot, proj_mid, proj_cold, tower_in, tower_out],
        scratch=[
            pltpu.VMEM((items, width), BF16),
            pltpu.VMEM((items, inner), BF16),
            pltpu.VMEM((items, width), BF16),
            pltpu.VMEM((3 * slots, width), BF16),
            pltpu.VMEM((reps, plan.rows, LANES), BF16),
        ],
        vmem=8 * groups - 8,
    )
    back = to_all(back)

    got = across_group(send, 1)
    ky, kx, kz, m1, m2 = plan.ky, plan.kx, plan.kz, plan.m1, plan.m2

    n1, n2 = plan.p1 // kx, plan.p2 // ky
    cuts = []
    for x in range(kx):
        cuts.append([(0, n1, [(0, x * n1), (1, x * n1)])])
    for y in range(ky):
        cuts.append([(0, n2, [(0, plan.p1 + y * n2), (1, plan.p1 + y * n2)])])
    parts = cut([keep, got], cuts)
    a_keep, a_send = parts[0], parts[1:kx]
    b_keep, b_send = parts[kx], parts[kx + 1 :]
    a_got = [across_rep(v, x + 1) for x, v in enumerate(a_send)]
    b_got = [across_group(v, 2 * (y + 1)) for y, v in enumerate(b_send)]
    k1, k2 = n1 // ky, n2 // kx
    na, nb = 1 + len(a_got), 1 + len(b_got)
    cuts = [[(0, k1, [(i, y * k1) for i in range(na)])] for y in range(ky)]
    cuts += [[(0, k2, [(na + i, x * k2) for i in range(nb)])] for x in range(kx)]
    parts = cut([a_keep, *a_got, b_keep, *b_got], cuts)
    a_keep, a_send = parts[0], parts[1:ky]
    b_keep, b_send = parts[ky], parts[ky + 1 :]
    a_got = [across_group(v, 2 * (y + 1)) for y, v in enumerate(a_send)]
    b_got = [across_rep(v, x + 1) for x, v in enumerate(b_send)]
    na, nb = 1 + len(a_got), 1 + len(b_got)
    cuts = [
        [
            (0, m1, [(i, z * m1) for i in range(na)]),
            (m1, m2, [(na + i, z * m2) for i in range(nb)]),
        ]
        for z in range(kz)
    ]
    parts = cut([a_keep, *a_got, b_keep, *b_got], cuts)
    z_got = [across_rep(parts[z], 2 * z) for z in range(1, kz)]
    mine = cut([parts[0], *z_got], [[(0, m1 + m2, [(i, 0) for i in range(kz)])]])[0]
    pieces = [mine] + [across_group(mine, t) for t in range(1, groups)]
    g_in, g_out, g_hot, g_mid, g_cold = call(
        functools.partial(final_body, plan, w_hot, w_mid, w_cold, cold_width),
        [
            sds((width, inner // reps), F32),
            sds((width // reps, inner), F32),
            sds((width // reps, w_hot), F32),
            sds((width // reps, w_mid), F32),
            sds((cold_width, width // reps), F32),
        ],
        pieces,
        scratch=[pltpu.VMEM((plan.rows, LANES), F32)],
        vmem=16,
    )

    q_keep, q_send = call(
        functools.partial(query_grad_body, groups),
        [sds((groups // 2, width, nq), BF16), sds((groups // 2, width, nq), BF16)],
        [vec, grad],
        vmem=16,
    )
    q_got = across_group(q_send, 1)
    own, *q_sends = call(
        query_core_body,
        [sds((width, nq), F32)] + [sds((width, nq), BF16)] * (ky - 1),
        [q_keep, q_got],
        vmem=16,
    )
    q_parts = [across_group(v, 2 * (y + 1)) for y, v in enumerate(q_sends)]
    query_grad = call(query_final_body, sds((nq, width), F32), [own, *q_parts], vmem=8)
    shapes = [table_hot.shape, table_mid.shape, table_cold.shape]
    o_hot, o_mid, o_cold = scatter_rows(served, back, proj_hot, shapes, cold_width)
    return (
        loss.reshape(nq),
        query_grad,
        o_hot,
        o_mid,
        o_cold,
        g_hot.T,
        g_mid.T,
        g_cold,
        g_in,
        g_out.T,
    )


def solution(mesh):
    split = P(AXES, None)
    deep = P(AXES, None, None)

    def body(*args):
        return local(mesh.shape["group"], mesh.shape["rep"], *args)

    return jax.shard_map(
        body,
        mesh=mesh,
        in_specs=(split, split, split, P(), P(), P(), P(), P(), split, P(AXES), deep, deep, deep),
        out_specs=(P(AXES), split, split, split, split) + (P(None, "rep"),) * 5,
        check_vma=False,
    )
```

time: 118 us -> 99.5 us (0.84)
  local copies, waits for them, and re-layouts: 14.3 us -> 5.34 us
  waiting for transfers between devices: 32.7 us -> 27.8 us
  Pallas kernels: 37.1 us -> 34.7 us
  starting transfers between devices: 31.9 us -> 30.1 us
    unnamed x68 -> x42, local copies, waits for them, and re-layouts: 14.3 us -> 5.34 us
    ppermute x17, waiting for transfers between devices: 24.2 us -> 19.3 us  [across_group(): return lax.ppermute(value, AXES, pairs)]
    pallas_call x12 -> x13, Pallas kernels: 32 us -> 29.5 us  [the longest x12 25.3 us: call(): pl.pallas_call(body, out_shape=out_shape, in_specs=[spec] * len(inputs) +...]
    ppermute x17, starting transfers between devices: 12.4 us -> 10.8 us  [across_group(): return lax.ppermute(value, AXES, pairs)]
  transfers between devices with their start and end apart: 24 -> 24, of which waited for: 8 -> 7; matrix products, arithmetic and copies ran while one was open for 0% -> 0% of each run, Pallas kernels for 10% -> 16%
where the time goes in v2:
time: 99.5 us; the launch traced here: 98.9 us
  Pallas kernels  34.7 us (35%)
  starting transfers between devices  30.1 us (30%)
  waiting for transfers between devices  27.8 us (28%)
  local copies, waits for them, and re-layouts  5.34 us (5%)
    pallas_call x12, Pallas kernels, call(): pl.pallas_call(body, out_shape=out_shape, in_specs=[spec] * len(inputs) +...  25.3 us
    ppermute x17, waiting for transfers between devices, across_group(): return lax.ppermute(value, AXES, pairs)  19.3 us
    all_to_all x2, starting transfers between devices, to_all(): return lax.all_to_all(each, AXES, 0, 0, tiled=True).reshape(rows.shape)  12.2 us
    ppermute x17, starting transfers between devices, across_group(): return lax.ppermute(value, AXES, pairs)  10.8 us
    ppermute x5, waiting for transfers between devices, across_rep(): return lax.ppermute(value, AXES, pairs)  8.51 us
    ppermute x5, starting transfers between devices, across_rep(): return lax.ppermute(value, AXES, pairs)  7.11 us
    unnamed x42, local copies, waits for them, and re-layouts  5.34 us
    pallas_call x1, Pallas kernels, scatter_rows(): pl.pallas_call(functools.partial(scatter_body, cold_width), grid=(steps,)...  5.14 us
  transfers between devices with their start and end apart: 24, of which 7 were waited for; matrix products, arithmetic and copies ran while one was open for 0% of the time, Pallas kernels for 16%

profile of v2, /device:TPU:0, one launch (start us, length us, event | category | flops | bytes accessed | tf_op | source)
XLA Modules:
  0.0 98.9 jit_solution(5617633449711076787)
XLA Ops:
  0.7 4.2 %gather_rows.1 = bf16[256,768]{1,0:T(8,128)(2,1)} custom-call(s32[3,1,256]{2,1,0:T(1,128)} %bitcast.17, bf16[1024,512]{1,0:T(8,128)(2,1)} %hot.1, bf16[4096,128]{1,0:T(8,128)(2,1)} %mid.1, bf16[4096,128]{1,0:T(8,128)(2,1)} %cold.1), custom_call_target="tpu_custom_call" | custom-call | tf_op jit(solution)/shard_map/gather_rows/pallas_call | solution.py:118
  5.0 7.3 %all-to-all-start = ((bf16[32,8,768]{2,1,0:T(8,128)(2,1)}), bf16[32,8,768]{2,1,0:T(8,128)(2,1)S(1)}, u32[]{:S(2)}, u32[]{:S(2)}) async-start(bf16[32,8,768]{2,1,0:T(8,128)(2,1)} %bitcast.23), calls=%async_computation | async-start | bytes 786432 | tf_op jit(solution)/shard_map/all_to_all | solution.py:519
  12.3 1.8 %collective-permute-start.4 = (bf16[512,256]{1,0:T(8,128)(2,1)S(1)}, bf16[512,256]{1,0:T(8,128)(2,1)S(1)}, u32[]{:S(2)}, u32[]{:S(2)}) collective-permute-start(bf16[512,256]{1,0:T(8,128)(2,1)S(1)} %copy-done.4), channel_id=1, source_target_pairs={{0,16},{1,17},{2,18},{3,19},{4,20},{5,21},{6,22},{7,23},{8,24},{9,... | collective-permute-start | bytes 786440 | tf_op jit(solution)/shard_map/ppermute | solution.py:511
  14.1 10.8 %collective-permute-done.4.rest_9_.refs_6_ = bf16[512,256]{1,0:T(8,128)(2,1)S(1)} collective-permute-done((bf16[512,256]{1,0:T(8,128)(2,1)S(1)}, bf16[512,256]{1,0:T(8,128)(2,1)S(1)}, u32[]{:S(2)}, u32[]{:S(2)}) %collective-permute-start.4) | collective-permute-done | bytes 262176 | tf_op jit(solution)/shard_map/ppermute | solution.py:511
  26.0 2.5 %collective-permute-done.1.rest_2_.refs_10_ = s32[1,512]{1,0:T(1,128)S(1)} collective-permute-done((s32[1,512]{1,0:T(1,128)S(1)}, s32[1,512]{1,0:T(1,128)S(1)}, u32[]{:S(2)}, u32[]{:S(2)}) %collective-permute-start.1) | collective-permute-done | bytes 2080 | tf_op jit(solution)/shard_map/ppermute | solution.py:511
  28.5 3.5 %shard_map.204.rest_4_ = bf16[1024,768]{1,0:T(8,128)(2,1)} custom-call(s32[1,4,1024]{2,1,0:T(4,128)} %item_slot.3, s32[1,4,1024]{2,1,0:T(4,128)} %item_block.3), custom_call_target="tpu_custom_call" | custom-call | tf_op jit(solution)/shard_map/pallas_call | solution.py:41
  32.1 1.4 %copy-done = bf16[1024,768]{1,0:T(8,128)(2,1)S(1)} copy-done((bf16[1024,768]{1,0:T(8,128)(2,1)S(1)}, bf16[1024,768]{1,0:T(8,128)(2,1)}, u32[]{:S(2)}) %copy-start) | copy-done | bytes 1572888
  33.5 7.0 %shard_map.205 = (bf16[1024,256]{1,0:T(8,128)(2,1)S(1)}, f32[1024,256]{1,0:T(8,128)S(1)}, bf16[1024,256]{1,0:T(8,128)(2,1)S(1)}, f32[8,768]{1,0:T(8,128)S(1)}, f32[1024,2048]{1,0:T(8,128)S(1)}) custom-call(bf16[256,768]{1,0:T(8,128)(2,1)S(1)} %bitcast.13, bf16[512,256]{1,0:T(8,128)(2,1)S(1)} %copy-done.2, bf16[128,256]{1,0:T(8,128)(2,1)S(1)} %copy-done.7, ...), custom_call_target="tpu_custom_call" | custom-call | tf_op jit(solution)/shard_map/pallas_call | solution.py:41
  41.6 1.2 %collective-permute-start.7 = (f32[8,768]{1,0:T(8,128)S(1)}, f32[8,768]{1,0:T(8,128)S(1)}, u32[]{:S(2)}, u32[]{:S(2)}) collective-permute-start(f32[8,768]{1,0:T(8,128)S(1)} %get-tuple-element.47.refs_0_), channel_id=1, source_target_pairs={{0,16},{1,17},{2,18},{3,19},{4,20},{5,21},{6,22},{7,23},{8,24},{9,... | collective-permute-start | bytes 73736 | tf_op jit(solution)/shard_map/ppermute | solution.py:511
  42.8 3.9 %shard_map.206 = (bf16[1024,1024]{1,0:T(8,128)(2,1)S(1)}, f32[1024,1024]{1,0:T(8,128)S(1)}, bf16[768,1024]{1,0:T(8,128)(2,1)S(1)}) custom-call(s32[1,4,1024]{2,1,0:T(4,128)S(1)} %copy-done.9, s32[1,4,1024]{2,1,0:T(4,128)S(1)} %copy-done.10, bf16[1024,256]{1,0:T(8,128)(2,1)S(1)} %get-tuple-element.49.pooled.refs_16_, bf16[256,1024]{1,0:T(8,128)(2,1)S(1)} %copy-done.1), custom_call_target="tpu_custom_call" | custom-call | tf_op jit(solution)/shard_map/pallas_call | solution.py:41
  48.8 6.6 %shard_map.207 = (f32[1,512]{1,0:T(1,128)}, bf16[1024,2048]{1,0:T(8,128)(2,1)S(1)}, bf16[2816,128]{1,0:T(8,128)(2,1)S(1)}, bf16[2816,128]{1,0:T(8,128)(2,1)}, bf16[256,512]{1,0:T(8,128)(2,1)S(1)}) custom-call(f32[8,768]{1,0:T(8,128)S(1)} %get-tuple-element.47.refs_0_, f32[8,768]{1,0:T(8,128)S(1)} %collective-permute-done.6.refs_1_, ...), custom_call_target="tpu_custom_call" | custom-call | tf_op jit(solution)/shard_map/pallas_call | solution.py:41
  55.9 2.1 %shard_map.208 = (bf16[2,256,512]{2,1,0:T(8,128)(2,1)S(1)}, bf16[2,256,512]{2,1,0:T(8,128)(2,1)}) custom-call(bf16[1024,256]{1,0:T(8,128)(2,1)S(1)} %get-tuple-element.55.vec, bf16[1024,2048]{1,0:T(8,128)(2,1)S(1)} %get-tuple-element.56.grad), custom_call_target="tpu_custom_call" | custom-call | tf_op jit(solution)/shard_map/pallas_call | solution.py:41
  57.9 4.8 %all-to-all-start.1 = ((bf16[32,8,512]{2,1,0:T(8,128)(2,1)}), bf16[32,8,512]{2,1,0:T(8,128)(2,1)S(1)}, u32[]{:S(2)}, u32[]{:S(2)}) async-start(bf16[32,8,512]{2,1,0:T(8,128)(2,1)} %bitcast.16), calls=%async_computation.1 | async-start | bytes 524288 | tf_op jit(solution)/shard_map/all_to_all | solution.py:519
  63.0 1.8 %collective-permute-start.12 = (bf16[768,128]{1,0:T(8,128)(2,1)S(1)}, bf16[768,128]{1,0:T(8,128)(2,1)S(1)}, u32[]{:S(2)}, u32[]{:S(2)}) collective-permute-start(bf16[768,128]{1,0:T(8,128)(2,1)S(1)} %get-tuple-element.68), channel_id=1, source_target_pairs={{0,1},{1,0},{2,3},{3,2},{4,5},{5,4},{6,7},{7,6},{8,9},{9,8},{10,11... | collective-permute-start | bytes 589832 | tf_op jit(solution)/shard_map/ppermute | solution.py:515
  64.8 1.5 %collective-permute-start.13 = (bf16[640,128]{1,0:T(8,128)(2,1)S(1)}, bf16[640,128]{1,0:T(8,128)(2,1)S(1)}, u32[]{:S(2)}, u32[]{:S(2)}) collective-permute-start(bf16[640,128]{1,0:T(8,128)(2,1)S(1)} %get-tuple-element.70), channel_id=1, source_target_pairs={{0,16},{1,17},{2,18},{3,19},{4,20},{5,21},{6,22},{7,23},{8,24},{9,... | collective-permute-start | bytes 491528 | tf_op jit(solution)/shard_map/ppermute | solution.py:511
  68.9 4.4 %collective-permute-done.13.refs_3_ = bf16[640,128]{1,0:T(8,128)(2,1)S(1)} collective-permute-done((bf16[640,128]{1,0:T(8,128)(2,1)S(1)}, bf16[640,128]{1,0:T(8,128)(2,1)S(1)}, u32[]{:S(2)}, u32[]{:S(2)}) %collective-permute-start.13) | collective-permute-done | bytes 163872 | tf_op jit(solution)/shard_map/ppermute | solution.py:511
  73.4 1.2 %collective-permute-start.14 = (bf16[384,128]{1,0:T(8,128)(2,1)S(1)}, bf16[384,128]{1,0:T(8,128)(2,1)S(1)}, u32[]{:S(2)}, u32[]{:S(2)}) collective-permute-start(bf16[384,128]{1,0:T(8,128)(2,1)S(1)} %get-tuple-element.72), channel_id=1, source_target_pairs={{0,16},{1,17},{2,18},{3,19},{4,20},{5,21},{6,22},{7,23},{8,24},{9,... | collective-permute-start | bytes 294920 | tf_op jit(solution)/shard_map/ppermute | solution.py:511
  75.4 3.6 %collective-permute-done.15.refs_3_ = bf16[320,128]{1,0:T(8,128)(2,1)S(1)} collective-permute-done((bf16[320,128]{1,0:T(8,128)(2,1)S(1)}, bf16[320,128]{1,0:T(8,128)(2,1)S(1)}, u32[]{:S(2)}, u32[]{:S(2)}) %collective-permute-start.15) | collective-permute-done | bytes 81952 | tf_op jit(solution)/shard_map/ppermute | solution.py:515
  79.0 1.6 %collective-permute-done.14.refs_1_ = bf16[384,128]{1,0:T(8,128)(2,1)S(1)} collective-permute-done((bf16[384,128]{1,0:T(8,128)(2,1)S(1)}, bf16[384,128]{1,0:T(8,128)(2,1)S(1)}, u32[]{:S(2)}, u32[]{:S(2)}) %collective-permute-start.14) | collective-permute-done | bytes 98336 | tf_op jit(solution)/shard_map/ppermute | solution.py:511
  80.6 1.5 %collective-permute-start.16 = (bf16[176,128]{1,0:T(8,128)(2,1)S(1)}, bf16[176,128]{1,0:T(8,128)(2,1)S(1)}, u32[]{:S(2)}, u32[]{:S(2)}) collective-permute-start(bf16[176,128]{1,0:T(8,128)(2,1)S(1)} %get-tuple-element.76), channel_id=1, source_target_pairs={{0,2},{1,3},{2,0},{3,1},{4,6},{5,7},{6,4},{7,5},{8,10},{9,11},{10,... | collective-permute-start | bytes 135176 | tf_op jit(solution)/shard_map/ppermute | solution.py:515
  82.1 2.0 %collective-permute-start.17 = (bf16[176,128]{1,0:T(8,128)(2,1)S(1)}, bf16[176,128]{1,0:T(8,128)(2,1)S(1)}, u32[]{:S(2)}, u32[]{:S(2)}) collective-permute-start(bf16[176,128]{1,0:T(8,128)(2,1)S(1)} %get-tuple-element.77), channel_id=1, source_target_pairs={{0,4},{1,5},{2,6},{3,7},{4,0},{5,1},{6,2},{7,3},{8,12},{9,13},{10,... | collective-permute-start | bytes 135176 | tf_op jit(solution)/shard_map/ppermute | solution.py:515
  85.1 2.5 %collective-permute-done.17.refs_2_ = bf16[176,128]{1,0:T(8,128)(2,1)S(1)} collective-permute-done((bf16[176,128]{1,0:T(8,128)(2,1)S(1)}, bf16[176,128]{1,0:T(8,128)(2,1)S(1)}, u32[]{:S(2)}, u32[]{:S(2)}) %collective-permute-start.17) | collective-permute-done | bytes 45088 | tf_op jit(solution)/shard_map/ppermute | solution.py:515
  87.6 2.4 %collective-permute-done.18.refs_3_ = bf16[176,128]{1,0:T(8,128)(2,1)S(1)} collective-permute-done((bf16[176,128]{1,0:T(8,128)(2,1)S(1)}, bf16[176,128]{1,0:T(8,128)(2,1)S(1)}, u32[]{:S(2)}, u32[]{:S(2)}) %collective-permute-start.18) | collective-permute-done | bytes 45088 | tf_op jit(solution)/shard_map/ppermute | solution.py:515
  91.9 5.1 %scatter_rows.1 = (f32[1,1024,512]{2,1,0:T(8,128)}, f32[4,1024,128]{2,1,0:T(8,128)}, f32[4,1024,128]{2,1,0:T(8,128)}) custom-call(s32[3,1,256]{2,1,0:T(1,128)S(1)} %bitcast.18, bf16[256,512]{1,0:T(8,128)(2,1)S(1)} %bitcast.15, bf16[512,256]{1,0:T(8,128)(2,1)S(1)} %copy-done.2), custom_call_target="tpu_custom_call" | custom-call | tf_op jit(solution)/shard_map/scatter_rows/pallas_call | solution.py:462
  (80 shorter events, 13.2 us)
Async XLA Ops:
  5.0 27.1 %all-to-all-start = ((bf16[32,8,768]{2,1,0:T(8,128)(2,1)}), bf16[32,8,768]{2,1,0:T(8,128)(2,1)S(1)}, u32[]{:S(2)}, u32[]{:S(2)}) async-start(bf16[32,8,768]{2,1,0:T(8,128)(2,1)} %bitcast.23), calls=%async_computation | async-start | bytes 786432 | tf_op jit(solution)/shard_map/all_to_all | solution.py:519
  12.3 12.6 %collective-permute-start.4 = (bf16[512,256]{1,0:T(8,128)(2,1)S(1)}, bf16[512,256]{1,0:T(8,128)(2,1)S(1)}, u32[]{:S(2)}, u32[]{:S(2)}) collective-permute-start(bf16[512,256]{1,0:T(8,128)(2,1)S(1)} %copy-done.4), channel_id=1, source_target_pairs={{0,16},{1,17},{2,18},{3,19},{4,20},{5,21},{6,22},{7,23},{8,24},{9,... | collective-permute-start | bytes 786440 | tf_op jit(solution)/shard_map/ppermute | solution.py:511
  14.1 17.9 %collective-permute-start.3 = (bf16[512,256]{1,0:T(8,128)(2,1)S(1)}, bf16[512,256]{1,0:T(8,128)(2,1)S(1)}, u32[]{:S(2)}, u32[]{:S(2)}) collective-permute-start(bf16[512,256]{1,0:T(8,128)(2,1)S(1)} %copy-done.4), channel_id=1, source_target_pairs={{0,8},{1,9},{2,10},{3,11},{4,12},{5,13},{6,14},{7,15},{8,0},{9,1},... | collective-permute-start | bytes 786440 | tf_op jit(solution)/shard_map/ppermute | solution.py:511
  24.9 7.1 %collective-permute-start.5 = (bf16[512,256]{1,0:T(8,128)(2,1)S(1)}, bf16[512,256]{1,0:T(8,128)(2,1)S(1)}, u32[]{:S(2)}, u32[]{:S(2)}) collective-permute-start(bf16[512,256]{1,0:T(8,128)(2,1)S(1)} %collective-permute-done.4.rest_9_.refs_6_), channel_id=1, source_target_pairs={{0,8},{1,9},{2,10},{3,11},{4,12},{5,13},{6,14},{7,15},{8,0},{9,1},... | collective-permute-start | bytes 786440 | tf_op jit(solution)/shard_map/ppermute | solution.py:511
  24.9 3.6 %collective-permute-start.1 = (s32[1,512]{1,0:T(1,128)S(1)}, s32[1,512]{1,0:T(1,128)S(1)}, u32[]{:S(2)}, u32[]{:S(2)}) collective-permute-start(s32[1,512]{1,0:T(1,128)S(1)} %bitcast.19), channel_id=1, source_target_pairs={{0,16},{1,17},{2,18},{3,19},{4,20},{5,21},{6,22},{7,23},{8,24},{9,... | collective-permute-start | bytes 6152 | tf_op jit(solution)/shard_map/ppermute | solution.py:511
  25.8 6.2 %collective-permute-start = (s32[1,512]{1,0:T(1,128)S(1)}, s32[1,512]{1,0:T(1,128)S(1)}, u32[]{:S(2)}, u32[]{:S(2)}) collective-permute-start(s32[1,512]{1,0:T(1,128)S(1)} %bitcast.20), channel_id=1, source_target_pairs={{0,8},{1,9},{2,10},{3,11},{4,12},{5,13},{6,14},{7,15},{8,0},{9,1},... | collective-permute-start | bytes 6152 | tf_op jit(solution)/shard_map/ppermute | solution.py:511
  28.5 3.5 %collective-permute-start.2 = (s32[1,512]{1,0:T(1,128)S(1)}, s32[1,512]{1,0:T(1,128)S(1)}, u32[]{:S(2)}, u32[]{:S(2)}) collective-permute-start(s32[1,512]{1,0:T(1,128)S(1)} %collective-permute-done.1.rest_2_.refs_10_), channel_id=1, source_target_pairs={{0,8},{1,9},{2,10},{3,11},{4,12},{5,13},{6,14},{7,15},{8,0},{9,1},... | collective-permute-start | bytes 6152 | tf_op jit(solution)/shard_map/ppermute | solution.py:511
  40.5 6.2 %collective-permute-start.8 = (f32[8,768]{1,0:T(8,128)S(1)}, f32[8,768]{1,0:T(8,128)S(1)}, u32[]{:S(2)}, u32[]{:S(2)}) collective-permute-start(f32[8,768]{1,0:T(8,128)S(1)} %get-tuple-element.47.refs_0_), channel_id=1, source_target_pairs={{0,24},{1,25},{2,26},{3,27},{4,28},{5,29},{6,30},{7,31},{8,16},{9,... | collective-permute-start | bytes 73736 | tf_op jit(solution)/shard_map/ppermute | solution.py:511
  41.6 5.1 %collective-permute-start.7 = (f32[8,768]{1,0:T(8,128)S(1)}, f32[8,768]{1,0:T(8,128)S(1)}, u32[]{:S(2)}, u32[]{:S(2)}) collective-permute-start(f32[8,768]{1,0:T(8,128)S(1)} %get-tuple-element.47.refs_0_), channel_id=1, source_target_pairs={{0,16},{1,17},{2,18},{3,19},{4,20},{5,21},{6,22},{7,23},{8,24},{9,... | collective-permute-start | bytes 73736 | tf_op jit(solution)/shard_map/ppermute | solution.py:511
  42.8 4.0 %collective-permute-start.6 = (f32[8,768]{1,0:T(8,128)S(1)}, f32[8,768]{1,0:T(8,128)S(1)}, u32[]{:S(2)}, u32[]{:S(2)}) collective-permute-start(f32[8,768]{1,0:T(8,128)S(1)} %get-tuple-element.47.refs_0_), channel_id=1, source_target_pairs={{0,8},{1,9},{2,10},{3,11},{4,12},{5,13},{6,14},{7,15},{8,0},{9,1},... | collective-permute-start | bytes 73736 | tf_op jit(solution)/shard_map/ppermute | solution.py:511
  55.4 7.4 %collective-permute-start.11 = (bf16[2816,128]{1,0:T(8,128)(2,1)}, bf16[2816,128]{1,0:T(8,128)(2,1)S(1)}, u32[]{:S(2)}, u32[]{:S(2)}) collective-permute-start(bf16[2816,128]{1,0:T(8,128)(2,1)} %get-tuple-element.66), channel_id=1, source_target_pairs={{0,8},{1,9},{2,10},{3,11},{4,12},{5,13},{6,14},{7,15},{8,0},{9,1},... | collective-permute-start | bytes 2162696 | tf_op jit(solution)/shard_map/ppermute | solution.py:511
  57.9 8.3 %collective-permute-start.9 = (bf16[2,256,512]{2,1,0:T(8,128)(2,1)}, bf16[2,256,512]{2,1,0:T(8,128)(2,1)S(1)}, u32[]{:S(2)}, u32[]{:S(2)}) collective-permute-start(bf16[2,256,512]{2,1,0:T(8,128)(2,1)} %get-tuple-element.58), channel_id=1, source_target_pairs={{0,8},{1,9},{2,10},{3,11},{4,12},{5,13},{6,14},{7,15},{8,0},{9,1},... | collective-permute-start | bytes 1572872 | tf_op jit(solution)/shard_map/ppermute | solution.py:511
  57.9 34.0 %all-to-all-start.1 = ((bf16[32,8,512]{2,1,0:T(8,128)(2,1)}), bf16[32,8,512]{2,1,0:T(8,128)(2,1)S(1)}, u32[]{:S(2)}, u32[]{:S(2)}) async-start(bf16[32,8,512]{2,1,0:T(8,128)(2,1)} %bitcast.16), calls=%async_computation.1 | async-start | bytes 524288 | tf_op jit(solution)/shard_map/all_to_all | solution.py:519
  63.0 10.3 %collective-permute-start.12 = (bf16[768,128]{1,0:T(8,128)(2,1)S(1)}, bf16[768,128]{1,0:T(8,128)(2,1)S(1)}, u32[]{:S(2)}, u32[]{:S(2)}) collective-permute-start(bf16[768,128]{1,0:T(8,128)(2,1)S(1)} %get-tuple-element.68), channel_id=1, source_target_pairs={{0,1},{1,0},{2,3},{3,2},{4,5},{5,4},{6,7},{7,6},{8,9},{9,8},{10,11... | collective-permute-start | bytes 589832 | tf_op jit(solution)/shard_map/ppermute | solution.py:515
  64.8 8.5 %collective-permute-start.13 = (bf16[640,128]{1,0:T(8,128)(2,1)S(1)}, bf16[640,128]{1,0:T(8,128)(2,1)S(1)}, u32[]{:S(2)}, u32[]{:S(2)}) collective-permute-start(bf16[640,128]{1,0:T(8,128)(2,1)S(1)} %get-tuple-element.70), channel_id=1, source_target_pairs={{0,16},{1,17},{2,18},{3,19},{4,20},{5,21},{6,22},{7,23},{8,24},{9,... | collective-permute-start | bytes 491528 | tf_op jit(solution)/shard_map/ppermute | solution.py:511
  68.2 28.8 %collective-permute-start.10 = (bf16[256,512]{1,0:T(8,128)(2,1)S(1)}, bf16[256,512]{1,0:T(8,128)(2,1)S(1)}, u32[]{:S(2)}, u32[]{:S(2)}) collective-permute-start(bf16[256,512]{1,0:T(8,128)(2,1)S(1)} %get-tuple-element.60), channel_id=1, source_target_pairs={{0,16},{1,17},{2,18},{3,19},{4,20},{5,21},{6,22},{7,23},{8,24},{9,... | collective-permute-start | bytes 786440 | tf_op jit(solution)/shard_map/ppermute | solution.py:511
  73.4 7.2 %collective-permute-start.14 = (bf16[384,128]{1,0:T(8,128)(2,1)S(1)}, bf16[384,128]{1,0:T(8,128)(2,1)S(1)}, u32[]{:S(2)}, u32[]{:S(2)}) collective-permute-start(bf16[384,128]{1,0:T(8,128)(2,1)S(1)} %get-tuple-element.72), channel_id=1, source_target_pairs={{0,16},{1,17},{2,18},{3,19},{4,20},{5,21},{6,22},{7,23},{8,24},{9,... | collective-permute-start | bytes 294920 | tf_op jit(solution)/shard_map/ppermute | solution.py:511
  74.6 4.4 %collective-permute-start.15 = (bf16[320,128]{1,0:T(8,128)(2,1)S(1)}, bf16[320,128]{1,0:T(8,128)(2,1)S(1)}, u32[]{:S(2)}, u32[]{:S(2)}) collective-permute-start(bf16[320,128]{1,0:T(8,128)(2,1)S(1)} %get-tuple-element.74), channel_id=1, source_target_pairs={{0,1},{1,0},{2,3},{3,2},{4,5},{5,4},{6,7},{7,6},{8,9},{9,8},{10,11... | collective-permute-start | bytes 245768 | tf_op jit(solution)/shard_map/ppermute | solution.py:515
  80.6 4.5 %collective-permute-start.16 = (bf16[176,128]{1,0:T(8,128)(2,1)S(1)}, bf16[176,128]{1,0:T(8,128)(2,1)S(1)}, u32[]{:S(2)}, u32[]{:S(2)}) collective-permute-start(bf16[176,128]{1,0:T(8,128)(2,1)S(1)} %get-tuple-element.76), channel_id=1, source_target_pairs={{0,2},{1,3},{2,0},{3,1},{4,6},{5,7},{6,4},{7,5},{8,10},{9,11},{10,... | collective-permute-start | bytes 135176 | tf_op jit(solution)/shard_map/ppermute | solution.py:515
  82.1 5.4 %collective-permute-start.17 = (bf16[176,128]{1,0:T(8,128)(2,1)S(1)}, bf16[176,128]{1,0:T(8,128)(2,1)S(1)}, u32[]{:S(2)}, u32[]{:S(2)}) collective-permute-start(bf16[176,128]{1,0:T(8,128)(2,1)S(1)} %get-tuple-element.77), channel_id=1, source_target_pairs={{0,4},{1,5},{2,6},{3,7},{4,0},{5,1},{6,2},{7,3},{8,12},{9,13},{10,... | collective-permute-start | bytes 135176 | tf_op jit(solution)/shard_map/ppermute | solution.py:515
  84.1 5.8 %collective-permute-start.18 = (bf16[176,128]{1,0:T(8,128)(2,1)S(1)}, bf16[176,128]{1,0:T(8,128)(2,1)S(1)}, u32[]{:S(2)}, u32[]{:S(2)}) collective-permute-start(bf16[176,128]{1,0:T(8,128)(2,1)S(1)} %get-tuple-element.78), channel_id=1, source_target_pairs={{0,6},{1,7},{2,4},{3,5},{4,2},{5,3},{6,0},{7,1},{8,14},{9,15},{10,... | collective-permute-start | bytes 135176 | tf_op jit(solution)/shard_map/ppermute | solution.py:515
  90.0 8.1 %collective-permute-start.21 = (bf16[176,128]{1,0:T(8,128)(2,1)S(1)}, bf16[176,128]{1,0:T(8,128)(2,1)S(1)}, u32[]{:S(2)}, u32[]{:S(2)}) collective-permute-start(bf16[176,128]{1,0:T(8,128)(2,1)S(1)} %shard_map.214.refs_0_), channel_id=1, source_target_pairs={{0,24},{1,25},{2,26},{3,27},{4,28},{5,29},{6,30},{7,31},{8,16},{9,... | collective-permute-start | bytes 135176 | tf_op jit(solution)/shard_map/ppermute | solution.py:511
  90.1 8.0 %collective-permute-start.20 = (bf16[176,128]{1,0:T(8,128)(2,1)S(1)}, bf16[176,128]{1,0:T(8,128)(2,1)S(1)}, u32[]{:S(2)}, u32[]{:S(2)}) collective-permute-start(bf16[176,128]{1,0:T(8,128)(2,1)S(1)} %shard_map.214.refs_0_), channel_id=1, source_target_pairs={{0,16},{1,17},{2,18},{3,19},{4,20},{5,21},{6,22},{7,23},{8,24},{9,... | collective-permute-start | bytes 135176 | tf_op jit(solution)/shard_map/ppermute | solution.py:511
  91.0 7.1 %collective-permute-start.19 = (bf16[176,128]{1,0:T(8,128)(2,1)S(1)}, bf16[176,128]{1,0:T(8,128)(2,1)S(1)}, u32[]{:S(2)}, u32[]{:S(2)}) collective-permute-start(bf16[176,128]{1,0:T(8,128)(2,1)S(1)} %shard_map.214.refs_0_), channel_id=1, source_target_pairs={{0,8},{1,9},{2,10},{3,11},{4,12},{5,13},{6,14},{7,15},{8,0},{9,1},... | collective-permute-start | bytes 135176 | tf_op jit(solution)/shard_map/ppermute | solution.py:511
  (21 other events, 295.5 us)
